TPU v7x, 32 devices: a whole 2x2x4 slice. The times are simulated.
32 devices in a mesh: rows: 4 (over y, x), tp: 8 (over z, core).
Axes of the slice: x: 2, y: 2, z: 4, core: 2. Of those that a mesh axis runs over, the one named last changes fastest.
Arguments:
- train_gate: float32 [3584, 14336], P('rows', 'tp'), may hold values from -0.125 to 0.125
- drift_gate: float32 [3584, 14336], P('rows', 'tp'), may hold values from -6 to 6
- spread_gate: float32 [3584, 14336], P('rows', 'tp'), may hold values from 0.1 to 10
- train_up: float32 [3584, 14336], P('rows', 'tp'), may hold values from -0.125 to 0.125
- drift_up: float32 [3584, 14336], P('rows', 'tp'), may hold values from -6 to 6
- spread_up: float32 [3584, 14336], P('rows', 'tp'), may hold values from 0.1 to 10
- norm_gain: float32 [3584], P('rows'), may hold values from 0.25 to 1.75
Outputs:
- serving_gate: bfloat16 [3584, 14336], P(None, 'tp')
- serving_up: bfloat16 [3584, 14336], P(None, 'tp')
- column_gate: float32 [14336], P('tp')
- column_up: float32 [14336], P('tp')
All inputs are finite; a program needn't handle non-finite values. Where the computation divides by a largest or mean magnitude, that divisor is 1e-20 or more.
Results may differ from a plain program's by a relative error of at most 0.001.
Values may be sent and summed in bfloat16 or wider, within the bound.
A program may use at most 128 MiB of HBM per device.

v0:
```python
import functools
import math

import jax
import jax.numpy as jnp
from jax import lax
from jax.experimental import pallas as pl
from jax.experimental.pallas import tpu as pltpu
from jax.sharding import PartitionSpec as P

learn_rate = 0.015
decay_rate = 0.1
tiny_value = 1e-08
MESH = pl.DeviceIdType.MESH
LANES = 128


def grid_of(rows):
    across = max(d for d in range(1, math.isqrt(rows) + 1) if rows % d == 0)
    return rows // across, across


def block_of(total, options):
    return next(b for b in options if total % b == 0)


def kernel(rows, width, step_rows, *refs):
    ins, gains, outs, columns = refs[:6], refs[6], refs[7:9], refs[9:11]
    stage, whole, peaks, gain = refs[11:15]
    in_sem, peak_send, peak_recv, first_send, first_recv, next_send, next_recv = refs[15:]
    tall, wide = grid_of(rows)
    share, total = ins[0].shape
    chunks = total // width
    me = lax.axis_index("rows")
    my_y, my_x = me // wide, lax.rem(me, wide)

    def along_x(k):
        return my_y * wide + lax.rem(my_x + k, wide)

    def along_y(k):
        return lax.rem(my_y + k, tall) * wide + my_x

    plans = ((along_x, wide, along_y, tall), (along_y, tall, along_x, wide))

    def cols(c):
        return pl.ds(pl.multiple_of(c * width, LANES), width)

    def part(m, owner, c):
        return outs[m].at[pl.ds(pl.multiple_of(owner * share, step_rows), share), cols(c)]

    def load(c, slot):
        return [
            pltpu.make_async_copy(ins[a].at[:, cols(c)], stage.at[slot, a], in_sem.at[slot, a])
            for a in range(6)
        ]

    def send(ref, peer, send_sem, recv_sem):
        return pltpu.make_async_remote_copy(
            src_ref=ref, dst_ref=ref, send_sem=send_sem, recv_sem=recv_sem,
            device_id={"rows": peer}, device_id_type=MESH,
        )

    def peak_copy(c, k):
        return send(peaks.at[c, me], lax.rem(me + k, rows), peak_send.at[c, k], peak_recv.at[c, k])

    def peak_arrival(c, k):
        source = lax.rem(me + rows - k, rows)
        return send(peaks.at[c, source], source, peak_send.at[c, k], peak_recv.at[c, k])

    def first_copy(m, c, k, owner):
        return send(part(m, owner, c), plans[m][0](k), first_send.at[c, m, k], first_recv.at[c, m, k])

    def next_copy(m, j, k, owner):
        block = outs[m].at[pl.ds(pl.multiple_of(owner * share, step_rows), share)]
        return send(block, plans[m][2](k), next_send.at[m, j, k], next_recv.at[m, j, k])

    def owner_first(m, j):
        near, size = plans[m][:2]
        return near(size - j) if j else me

    def owner_next(m, j, k):
        y, x = my_y, my_x
        if m == 0:
            y, x = lax.rem(y + tall - k, tall), lax.rem(x + wide - j, wide)
        else:
            y, x = lax.rem(y + tall - j, tall), lax.rem(x + wide - k, wide)
        return y * wide + x

    for copy in load(0, 0):
        copy.start()

    @pl.when(chunks > 1)
    def _():
        for copy in load(min(1, chunks - 1), 1):
            copy.start()

    barrier = pltpu.get_barrier_semaphore()
    for k in range(1, rows):
        pl.semaphore_signal(
            barrier, inc=1, device_id={"rows": lax.rem(me + k, rows)}, device_id_type=MESH
        )
    pl.semaphore_wait(barrier, rows - 1)

    for start in range(0, share, LANES):
        count = min(LANES, share - start)
        line = gains[pl.ds(start, count)].reshape(1, count)
        gain[pl.ds(start, count), :] = jnp.broadcast_to(line, (LANES, count)).T

    def update(c):
        slot = lax.rem(c, 2)
        for copy in load(c, slot):
            copy.wait()

        def step(i, most):
            at = pl.ds(pl.multiple_of(i * step_rows, step_rows), step_rows)
            g = gain[at, :]
            found = []
            for m in range(2):
                for t in range(width // LANES):
                    lane = pl.ds(t * LANES, LANES)
                    train, drift, spread = (stage[slot, 3 * m + a, at, lane] for a in range(3))
                    new = train - learn_rate * (
                        drift / (jnp.sqrt(spread) + tiny_value) + decay_rate * train
                    )
                    new = new * g
                    whole[slot, m, at, lane] = new
                    tops = jnp.max(jnp.abs(new).reshape(step_rows // 8, 8, LANES), axis=0)
                    found.append(jnp.maximum(most[len(found)], tops))
            return tuple(found)

        zero = jnp.zeros((8, LANES), jnp.float32)
        most = lax.fori_loop(0, share // step_rows, step, (zero,) * (2 * (width // LANES)))
        for m in range(2):
            for t in range(width // LANES):
                peaks[c, me, m : m + 1, pl.ds(t * LANES, LANES)] = jnp.max(
                    most[m * (width // LANES) + t], axis=0, keepdims=True
                )
        for k in range(1, rows):
            peak_copy(c, k).start()

    def finish(c):
        slot = lax.rem(c, 2)
        for k in range(1, rows):
            peak_arrival(c, k).wait_recv()
        scale = peaks[c, 0]
        for r in range(1, rows):
            scale = jnp.maximum(scale, peaks[c, r])
        for m in range(2):
            columns[m][cols(c)] = scale[m]
        inverse = 1.0 / scale
        for m in range(2):
            factor = inverse[m : m + 1, :]

            def step(i, carry, m=m, factor=factor):
                at = pl.ds(pl.multiple_of(i * step_rows, step_rows), step_rows)
                to = pl.ds(pl.multiple_of(me * share + i * step_rows, step_rows), step_rows)
                outs[m][to, cols(c)] = (whole[slot, m, at, :] * factor).astype(jnp.bfloat16)
                return carry

            lax.fori_loop(0, share // step_rows, step, 0)
            for k in range(1, plans[m][1]):
                first_copy(m, c, k, me).start()

    update(0)

    def body(c, carry):
        @pl.when(c + 1 < chunks)
        def _():
            for copy in load(c + 1, lax.rem(c + 1, 2)):
                copy.start()

        update(c)
        finish(c - 1)
        return carry

    lax.fori_loop(1, chunks, body, 0)
    finish(chunks - 1)

    for m in range(2):
        for k in range(1, plans[m][3]):
            next_copy(m, 0, k, me).start()

    for j in range(1, max(tall, wide)):
        for m in range(2):
            if j < plans[m][1]:
                owner = owner_first(m, j)

                def arrive(c, carry, m=m, j=j, owner=owner):
                    first_copy(m, c, j, owner).wait_recv()
                    return carry

                lax.fori_loop(0, chunks, arrive, 0)
                for k in range(1, plans[m][3]):
                    next_copy(m, j, k, owner).start()

    def drain(c, carry):
        for k in range(1, rows):
            peak_copy(c, k).wait_send()
        for m in range(2):
            for k in range(1, plans[m][1]):
                first_copy(m, c, k, me).wait_send()
        return carry

    lax.fori_loop(0, chunks, drain, 0)
    for m in range(2):
        for j in range(plans[m][1]):
            for k in range(1, plans[m][3]):
                next_copy(m, j, k, owner_first(m, j)).wait_send()
                next_copy(m, j, k, owner_next(m, j, k)).wait_recv()


def settle(pieces, *arrays):
    def body(*refs):
        count = len(arrays)
        sem = refs[-1]
        copies = []
        for a in range(count):
            parts = pieces if arrays[a].ndim > 1 else 1
            tall = arrays[a].shape[0] // parts
            for p in range(parts):
                at = pl.ds(p * tall, tall)
                copies.append(
                    pltpu.make_async_copy(refs[a].at[at], refs[count + a].at[at], sem.at[a, p])
                )
        for copy in copies:
            copy.start()
        for copy in copies:
            copy.wait()

    return pl.pallas_call(
        body,
        out_shape=tuple(jax.ShapeDtypeStruct(a.shape, a.dtype) for a in arrays),
        in_specs=[pl.BlockSpec(memory_space=pl.ANY)] * len(arrays),
        out_specs=(pl.BlockSpec(memory_space=pltpu.HBM),) * len(arrays),
        scratch_shapes=[pltpu.SemaphoreType.DMA((len(arrays), pieces))],
        compiler_params=pltpu.CompilerParams(vmem_limit_bytes=SMALL),
    )(*arrays)


def solution(mesh):
    rows = mesh.shape["rows"]

    def per_device(*args):
        arrays, norm_gain = args[:6], args[6]
        share, total = arrays[0].shape
        width = block_of(total, (LANES,))
        step_rows = block_of(share, (32, 16))
        chunks = total // width
        most = max(grid_of(rows))
        served = pltpu.VMEM((rows * share, total), jnp.bfloat16)
        column = pltpu.VMEM((total,), jnp.float32)
        dma = pltpu.SemaphoreType.DMA
        serving_gate, serving_up, column_gate, column_up = pl.pallas_call(
            functools.partial(kernel, rows, width, step_rows),
            out_shape=(served, served, column, column),
            in_specs=[pl.BlockSpec(memory_space=pltpu.HBM)] * 6
            + [pl.BlockSpec(memory_space=pltpu.VMEM)],
            out_specs=(pl.BlockSpec(memory_space=pltpu.VMEM),) * 4,
            scratch_shapes=[
                pltpu.VMEM((2, 6, share, width), jnp.float32),
                pltpu.VMEM((2, 2, share, width), jnp.float32),
                pltpu.VMEM((chunks, rows, 2, width), jnp.float32),
                pltpu.VMEM((share, LANES), jnp.float32),
                dma((2, 6)),
                dma((chunks, rows)),
                dma((chunks, rows)),
                dma((chunks, 2, most)),
                dma((chunks, 2, most)),
                dma((2, most, most)),
                dma((2, most, most)),
            ],
            compiler_params=pltpu.CompilerParams(
                collective_id=0, has_side_effects=True, vmem_limit_bytes=VMEM_LIMIT
            ),
        )(*arrays, norm_gain)
        return settle(2 * rows, serving_gate, serving_up, column_gate, column_up)

    split = P("rows", "tp")
    return jax.shard_map(
        per_device,
        mesh=mesh,
        in_specs=(split,) * 6 + (P("rows"),),
        out_specs=(P(None, "tp"), P(None, "tp"), P("tp"), P("tp")),
        check_vma=False,
    )


VMEM_LIMIT = 34 * 1024 * 1024
SMALL = 1024 * 1024
```

profile of v0, /device:TPU:1, one launch (start us, length us, event | category | flops | bytes accessed | tf_op | source)
XLA Modules:
  0.0 226.2 jit_solution(11353789660873296048)
XLA Ops:
  0.6 216.7 %shard_map.102 = (bf16[3584,1792]{1,0:T(8,128)(2,1)S(1)}, bf16[3584,1792]{1,0:T(8,128)(2,1)S(1)}, f32[1792]{0:T(1024)S(1)}, f32[1792]{0:T(1024)S(1)}) custom-call(f32[896,1792]{1,0:T(8,128)} %refs_0_.1, f32[896,1792]{1,0:T(8,128)} %refs_1_.1, f32[896,1792]{1,0:T(8,128)} %refs_2_.1, f32[896,1792]{1,0:T(8,128)} %refs_3_.1, f32[896,1792]{1,0:T(8,128)} %refs_4_.1, ...), custom_call_target="tpu_custom_call" | custom-call | tf_op jit(solution)/shard_map/pallas_call | solution.py:253
  217.4 8.8 %shard_map.103 = (bf16[3584,1792]{1,0:T(8,128)(2,1)}, bf16[3584,1792]{1,0:T(8,128)(2,1)}, f32[1792]{0:T(1024)}, f32[1792]{0:T(1024)}) custom-call(bf16[3584,1792]{1,0:T(8,128)(2,1)S(1)} %get-tuple-element.8.refs_0_, bf16[3584,1792]{1,0:T(8,128)(2,1)S(1)} %get-tuple-element.9.refs_1_, f32[1792]{0:T(1024)S(1)} %get-tuple-element.10.refs_2_, ...), custom_call_target="tpu_custom_call" | custom-call | tf_op jit(solution)/shard_map/pallas_call | solution.py:230
where the time goes:
time: 228 us; the launch traced here: 226 us
  Pallas kernels  226 us (99%)
    pallas_call x1, Pallas kernels, per_device(): pl.pallas_call(functools.partial(kernel, rows, width, step_rows), out_sha...  217 us
    pallas_call x1, Pallas kernels, settle(): pl.pallas_call(body, out_shape=tuple((jax.ShapeDtypeStruct(a.shape, a.dty...  8.82 us

commit v1 on v0

v1 whole, which is shorter than its diff:
```python
import functools
import math

import jax
import jax.numpy as jnp
from jax import lax
from jax.experimental import pallas as pl
from jax.experimental.pallas import tpu as pltpu
from jax.sharding import PartitionSpec as P

learn_rate = 0.015
decay_rate = 0.1
tiny_value = 1e-08
MESH = pl.DeviceIdType.MESH
LANES = 128


def grid_of(rows):
    across = max(d for d in range(1, math.isqrt(rows) + 1) if rows % d == 0)
    return rows // across, across


def block_of(total, options):
    return next(b for b in options if total % b == 0)


def place(rows):
    tall, wide = grid_of(rows)
    me = lax.axis_index("rows")
    turn = lax.rem(lax.axis_index("tp"), 2) if tall == wide else 0
    return me, me // wide, lax.rem(me, wide), turn


def kernel(rows, width, step_rows, late_chunks, *refs):
    ins, gains, outs, columns = refs[:6], refs[6], refs[7:9], refs[9:11]
    late, rest = (refs[11], refs[12:]) if late_chunks else (None, refs[11:])
    stage, whole, peaks, gain = rest[:4]
    in_sem, peak_send, peak_recv, first_send, first_recv, next_send, next_recv = rest[4:]
    tall, wide = grid_of(rows)
    share, total = ins[0].shape
    chunks = total // width
    kept = chunks - late_chunks
    me, my_y, my_x, turn = place(rows)
    lead = (turn, 1 - turn)
    sizes = ((wide, tall), (tall, wide))

    def along_x(k):
        return my_y * wide + lax.rem(my_x + k, wide)

    def along_y(k):
        return lax.rem(my_y + k, tall) * wide + my_x

    def first_peer(m, k):
        return (1 - lead[m]) * along_x(k) + lead[m] * along_y(k)

    def next_peer(m, k):
        return (1 - lead[m]) * along_y(k) + lead[m] * along_x(k)

    def owner_next(m, j, k):
        down = (1 - lead[m]) * k + lead[m] * j
        left = (1 - lead[m]) * j + lead[m] * k
        return lax.rem(my_y + tall - down, tall) * wide + lax.rem(my_x + wide - left, wide)

    def owner_first(m, j):
        return first_peer(m, sizes[m][0] - j) if j else me

    def cols(c):
        return pl.ds(pl.multiple_of(c * width, LANES), width)

    def part(m, owner, c):
        return outs[m].at[pl.ds(pl.multiple_of(owner * share, step_rows), share), cols(c)]

    def load(m, c):
        slot = lax.rem(c, 2)
        return [
            pltpu.make_async_copy(
                ins[3 * m + a].at[:, cols(c)], stage.at[slot, 3 * m + a], in_sem.at[slot, 3 * m + a]
            )
            for a in range(3)
        ]

    def send(src, dst, peer, send_sem, recv_sem):
        return pltpu.make_async_remote_copy(
            src_ref=src, dst_ref=dst, send_sem=send_sem, recv_sem=recv_sem,
            device_id={"rows": peer}, device_id_type=MESH,
        )

    def peak_copy(m, c, k, source, peer):
        ref = peaks.at[m, c, source]
        return send(ref, ref, peer, peak_send.at[m, c, k], peak_recv.at[m, c, k])

    def first_copy(m, c, k, owner, kept_part=True):
        src = part(m, owner, c)
        dst = src if kept_part else late.at[:, cols(c - kept)]
        return send(src, dst, first_peer(m, k), first_send.at[c, m, k], first_recv.at[c, m, k])

    def next_copy(m, j, c, k, owner):
        ref = part(m, owner, c)
        return send(ref, ref, next_peer(m, k), next_send.at[j, c, m, k], next_recv.at[j, c, m, k])

    for copy in load(0, 0):
        copy.start()

    barrier = pltpu.get_barrier_semaphore()
    for k in range(1, rows):
        pl.semaphore_signal(
            barrier, inc=1, device_id={"rows": lax.rem(me + k, rows)}, device_id_type=MESH
        )

    for start in range(0, share, LANES):
        count = min(LANES, share - start)
        line = gains[pl.ds(start, count)].reshape(1, count)
        gain[pl.ds(start, count), :] = jnp.broadcast_to(line, (LANES, count)).T

    for copy in load(1, 0):
        copy.start()

    pl.semaphore_wait(barrier, rows - 1)

    def update(m, c):
        slot = lax.rem(c, 2)
        for copy in load(m, c):
            copy.wait()

        @pl.when(c + 1 < chunks)
        def _():
            for copy in load(m, c + 1):
                copy.start()

        def step(i, most):
            at = pl.ds(pl.multiple_of(i * step_rows, step_rows), step_rows)
            g = gain[at, :]
            found = []
            for t in range(width // LANES):
                lane = pl.ds(t * LANES, LANES)
                train, drift, spread = (stage[slot, 3 * m + a, at, lane] for a in range(3))
                new = train - learn_rate * (
                    drift / (jnp.sqrt(spread) + tiny_value) + decay_rate * train
                )
                new = new * g
                whole[slot, m, at, lane] = new
                tops = jnp.max(jnp.abs(new).reshape(step_rows // 8, 8, LANES), axis=0)
                found.append(jnp.maximum(most[t], tops))
            return tuple(found)

        zero = jnp.zeros((8, LANES), jnp.float32)
        most = lax.fori_loop(0, share // step_rows, step, (zero,) * (width // LANES))
        for t in range(width // LANES):
            peaks[m, c, me, :, pl.ds(t * LANES, LANES)] = jnp.max(most[t], axis=0, keepdims=True)
        for k in range(1, rows):
            peak_copy(m, c, k, me, lax.rem(me + k, rows)).start()

    def finish(m, c):
        slot = lax.rem(c, 2)
        for k in range(1, rows):
            source = lax.rem(me + rows - k, rows)
            peak_copy(m, c, k, source, source).wait_recv()
        scale = peaks[m, c, 0]
        for r in range(1, rows):
            scale = jnp.maximum(scale, peaks[m, c, r])
        columns[m][cols(c)] = scale[0]
        factor = 1.0 / scale

        def step(i, carry):
            at = pl.ds(pl.multiple_of(i * step_rows, step_rows), step_rows)
            to = pl.ds(pl.multiple_of(me * share + i * step_rows, step_rows), step_rows)
            outs[m][to, cols(c)] = (whole[slot, m, at, :] * factor).astype(jnp.bfloat16)
            return carry

        lax.fori_loop(0, share // step_rows, step, 0)
        for k in range(1, sizes[m][0]):
            if m == 0 and late_chunks:

                @pl.when(c < kept)
                def _(k=k):
                    first_copy(m, c, k, me).start()

                @pl.when(c >= kept)
                def _(k=k):
                    first_copy(m, c, k, me, False).start()

            else:
                first_copy(m, c, k, me).start()
        for k in range(1, sizes[m][1]):
            next_copy(m, 0, c, k, me).start()

    def body(c, carry):
        update(0, c)

        @pl.when(c >= 2)
        def _():
            finish(1, c - 2)

        update(1, c)

        @pl.when(c >= 1)
        def _():
            finish(0, c - 1)

        return carry

    lax.fori_loop(0, chunks, body, 0)
    if chunks > 1:
        finish(1, chunks - 2)
    finish(0, chunks - 1)
    finish(1, chunks - 1)

    def forward(m, j, c):
        owner = owner_first(m, j)
        first_copy(m, c, j, owner).wait_recv()
        for k in range(1, sizes[m][1]):
            next_copy(m, j, c, k, owner).start()

    def relay(low, high, late_part):
        def step(c, carry):
            for j in range(1, max(tall, wide)):
                for m in range(2):
                    if j < sizes[m][0]:
                        if m == 0 and late_part:
                            first_copy(m, c, j, me, False).wait_recv()
                        else:
                            forward(m, j, c)
            return carry

        lax.fori_loop(low, high, step, 0)

    relay(0, kept, False)
    if late_chunks:
        relay(kept, chunks, True)

    def drain(c, carry, kept_part=True):
        for m in range(2):
            for k in range(1, rows):
                peak_copy(m, c, k, me, lax.rem(me + k, rows)).wait_send()
            for k in range(1, sizes[m][0]):
                first_copy(m, c, k, me, kept_part or m == 1).wait_send()
            for j in range(sizes[m][0]):
                if j == 0 or m == 1 or kept_part:
                    for k in range(1, sizes[m][1]):
                        next_copy(m, j, c, k, owner_first(m, j)).wait_send()
                        next_copy(m, j, c, k, owner_next(m, j, k)).wait_recv()
        return carry

    lax.fori_loop(0, kept, drain, 0)
    if late_chunks:
        lax.fori_loop(kept, chunks, functools.partial(drain, kept_part=False), 0)


def settle(rows, late_cols, pieces, arrays, late=None):
    ins = arrays + ((late,) if late_cols else ())
    count = len(ins)

    def body(*refs):
        sem = refs[-1]
        copies = []

        def add(src, dst):
            copies.append(pltpu.make_async_copy(src, dst, sem.at[len(copies)]))

        for a in range(len(arrays)):
            src, dst = refs[a], refs[count + a]
            if arrays[a].ndim == 1:
                add(src, dst)
                continue
            tall_share = arrays[a].shape[0] // rows
            tall = tall_share // pieces
            own = arrays[a].shape[1] - late_cols
            if a or not late_cols:
                for p in range(rows * pieces):
                    at = pl.ds(p * tall, tall)
                    add(src.at[at], dst.at[at])
                continue
            me, near, side, far = around(rows)
            for owner, whole in ((me, True), (side, True), (near, False), (far, False)):
                for p in range(pieces):
                    at = pl.ds(pl.multiple_of(owner * tall_share + p * tall, 16), tall)
                    if whole:
                        add(src.at[at], dst.at[at])
                    else:
                        add(src.at[at, pl.ds(0, own)], dst.at[at, pl.ds(0, own)])
            at = pl.ds(pl.multiple_of(near * tall_share, 16), tall_share)
            add(refs[count - 1], dst.at[at, pl.ds(own, late_cols)])
        for copy in copies:
            copy.start()
        for copy in copies:
            copy.wait()

    size = sum(a.size * a.dtype.itemsize for a in arrays)
    return pl.pallas_call(
        body,
        out_shape=tuple(jax.ShapeDtypeStruct(a.shape, a.dtype) for a in arrays),
        in_specs=[pl.BlockSpec(memory_space=pl.ANY)] * count,
        out_specs=(pl.BlockSpec(memory_space=pltpu.HBM),) * len(arrays),
        scratch_shapes=[pltpu.SemaphoreType.DMA((2 * rows * pieces + 3,))],
        compiler_params=pltpu.CompilerParams(vmem_limit_bytes=SMALL),
        cost_estimate=pl.CostEstimate(flops=4 * size, bytes_accessed=2 * size, transcendentals=0),
    )(*ins)


def around(rows):
    me, y, x, turn = place(rows)
    by_x, by_y = y * 2 + (1 - x), (1 - y) * 2 + x
    near = (1 - turn) * by_x + turn * by_y
    side = (1 - turn) * by_y + turn * by_x
    return me, near, side, (1 - y) * 2 + (1 - x)


def complete(rows, served, piece):
    share, late_cols = piece.shape
    own = served.shape[1] - late_cols

    def body(_, src, dst, sem):
        far = around(rows)[3]
        at = pl.ds(pl.multiple_of(far * share, 16), share)
        copy = pltpu.make_async_copy(src, dst.at[at, pl.ds(own, late_cols)], sem)
        copy.start()
        copy.wait()

    return pl.pallas_call(
        body,
        out_shape=jax.ShapeDtypeStruct(served.shape, served.dtype),
        in_specs=[pl.BlockSpec(memory_space=pltpu.HBM), pl.BlockSpec(memory_space=pl.ANY)],
        out_specs=pl.BlockSpec(memory_space=pltpu.HBM),
        scratch_shapes=[pltpu.SemaphoreType.DMA],
        input_output_aliases={0: 0},
        compiler_params=pltpu.CompilerParams(vmem_limit_bytes=SMALL),
    )(served, piece)


def solution(mesh):
    rows, lanes = mesh.shape["rows"], mesh.shape["tp"]

    def per_device(*args):
        arrays, norm_gain = args[:6], args[6]
        share, total = arrays[0].shape
        width = block_of(total, (LANES,))
        step_rows = block_of(share, (32, 16))
        chunks = total // width
        most = max(grid_of(rows))
        late_chunks = LATE if grid_of(rows) == (2, 2) and chunks > LATE else 0
        late_cols = late_chunks * width
        served = pltpu.VMEM((rows * share, total), jnp.bfloat16)
        column = pltpu.VMEM((total,), jnp.float32)
        late = (pltpu.VMEM((share, late_cols), jnp.bfloat16),) if late_chunks else ()
        dma = pltpu.SemaphoreType.DMA
        got = pl.pallas_call(
            functools.partial(kernel, rows, width, step_rows, late_chunks),
            out_shape=(served, served, column, column) + late,
            in_specs=[pl.BlockSpec(memory_space=pltpu.HBM)] * 6
            + [pl.BlockSpec(memory_space=pltpu.VMEM)],
            out_specs=(pl.BlockSpec(memory_space=pltpu.VMEM),) * (4 + len(late)),
            scratch_shapes=[
                pltpu.VMEM((2, 6, share, width), jnp.float32),
                pltpu.VMEM((2, 2, share, width), jnp.float32),
                pltpu.VMEM((2, chunks, rows, 1, width), jnp.float32),
                pltpu.VMEM((share, LANES), jnp.float32),
                dma((2, 6)),
                dma((2, chunks, rows)),
                dma((2, chunks, rows)),
                dma((chunks, 2, most)),
                dma((chunks, 2, most)),
                dma((most, chunks, 2, most)),
                dma((most, chunks, 2, most)),
            ],
            compiler_params=pltpu.CompilerParams(
                collective_id=0, has_side_effects=True, vmem_limit_bytes=VMEM_LIMIT
            ),
        )(*arrays, norm_gain)
        if not late_chunks:
            return settle(rows, 0, 2, got)
        hops = [
            (r * lanes + t, (r ^ (1 if t % 2 else 2)) * lanes + t)
            for r in range(rows)
            for t in range(lanes)
        ]
        piece = lax.ppermute(got[4], ("rows", "tp"), hops)
        done = settle(rows, late_cols, 2, got[:4], got[4])
        return (complete(rows, done[0], piece),) + tuple(done[1:])

    split = P("rows", "tp")
    return jax.shard_map(
        per_device,
        mesh=mesh,
        in_specs=(split,) * 6 + (P("rows"),),
        out_specs=(P(None, "tp"), P(None, "tp"), P("tp"), P("tp")),
        check_vma=False,
    )


LATE = 4
VMEM_LIMIT = 36 * 1024 * 1024
SMALL = 1024 * 1024
```

time: 228 us -> 227 us (level)
  Pallas kernels: 226 us -> 220 us
  waiting for transfers between devices: 0 us -> 2.98 us
    pallas_call x1 -> x2, Pallas kernels: 217 us -> 212 us  [the longest x1 211 us: per_device(): pl.pallas_call(functools.partial(kernel, rows, width, step_rows, late_chu...]
    ppermute x0 -> x1, waiting for transfers between devices: none -> 2.98 us  [per_device(): piece = lax.ppermute(got[4], ('rows', 'tp'), hops)]
  transfers between devices with their start and end apart: 0 -> 1, of which waited for: 0 -> 1; matrix products, arithmetic and copies ran while one was open for 0% -> 0% of each run, Pallas kernels for 0% -> 4%
where the time goes in v1:
time: 227 us; the launch traced here: 225 us
  Pallas kernels  220 us (97%)
  waiting for transfers between devices  2.98 us (1%)
    pallas_call x1, Pallas kernels, per_device(): pl.pallas_call(functools.partial(kernel, rows, width, step_rows, late_chu...  211 us
    pallas_call x1, Pallas kernels, settle(): pl.pallas_call(body, out_shape=tuple((jax.ShapeDtypeStruct(a.shape, a.dty...  8.42 us
  transfers between devices with their start and end apart: 1, of which 1 were waited for; matrix products, arithmetic and copies ran while one was open for 0% of the time, Pallas kernels for 4%

profile of v1, /device:TPU:1, one launch (start us, length us, event | category | flops | bytes accessed | tf_op | source)
XLA Modules:
  0.0 225.2 jit_solution(17434219672455962210)
XLA Ops:
  0.6 211.0 %shard_map.102 = (bf16[3584,1792]{1,0:T(8,128)(2,1)S(1)}, bf16[3584,1792]{1,0:T(8,128)(2,1)S(1)}, f32[1792]{0:T(1024)S(1)}, f32[1792]{0:T(1024)S(1)}, bf16[896,512]{1,0:T(8,128)(2,1)S(1)}) custom-call(f32[896,1792]{1,0:T(8,128)} %refs_0_.1, f32[896,1792]{1,0:T(8,128)} %refs_1_.1, f32[896,1792]{1,0:T(8,128)} %refs_2_.1, f32[896,1792]{1,0:T(8,128)} %refs_3_.1, ...), custom_call_target="tpu_custom_call" | custom-call | tf_op jit(solution)/shard_map/pallas_call | solution.py:346
  211.6 1.2 collective-permute-start
  212.8 8.4 %shard_map.103 = (bf16[3584,1792]{1,0:T(8,128)(2,1)}, bf16[3584,1792]{1,0:T(8,128)(2,1)}, f32[1792]{0:T(1024)}, f32[1792]{0:T(1024)}) custom-call(bf16[3584,1792]{1,0:T(8,128)(2,1)S(1)} %get-tuple-element.13.refs_0_, bf16[3584,1792]{1,0:T(8,128)(2,1)S(1)} %get-tuple-element.14.refs_1_, f32[1792]{0:T(1024)S(1)} %get-tuple-element.15.refs_2_, ...), custom_call_target="tpu_custom_call" | custom-call | flops 102817792 | bytes 51408896 | tf_op jit(solution)/shard_map/pallas_call | solution.py:289
  221.3 3.0 %collective-permute-done.src = bf16[896,512]{1,0:T(8,128)(2,1)S(1)} collective-permute-done((bf16[896,512]{1,0:T(8,128)(2,1)S(1)}, bf16[896,512]{1,0:T(8,128)(2,1)S(1)}, u32[]{:S(2)}, u32[]{:S(2)}) %collective-permute-start) | collective-permute-done | bytes 917536 | tf_op jit(solution)/shard_map/ppermute | solution.py:376
  224.2 0.9 shard_map.104
Async XLA Ops:
  211.6 12.6 %collective-permute-start = (bf16[896,512]{1,0:T(8,128)(2,1)S(1)}, bf16[896,512]{1,0:T(8,128)(2,1)S(1)}, u32[]{:S(2)}, u32[]{:S(2)}) collective-permute-start(bf16[896,512]{1,0:T(8,128)(2,1)S(1)} %get-tuple-element.17.refs_4_), channel_id=1, source_target_pairs={{0,16},{1,9},{2,18},{3,11},{4,20},{5,13},{6,22},{7,15},{8,24},{9,1... | collective-permute-start | bytes 2752520 | tf_op jit(solution)/shard_map/ppermute | solution.py:376

commit v2 on v1

v2 whole, which is shorter than its diff:
```python
import functools
import math

import jax
import jax.numpy as jnp
from jax import lax
from jax.experimental import pallas as pl
from jax.experimental.pallas import tpu as pltpu
from jax.sharding import PartitionSpec as P

learn_rate = 0.015
decay_rate = 0.1
tiny_value = 1e-08
MESH = pl.DeviceIdType.MESH
LANES = 128


def grid_of(rows):
    across = max(d for d in range(1, math.isqrt(rows) + 1) if rows % d == 0)
    return rows // across, across


def block_of(total, options):
    return next(b for b in options if total % b == 0)


def place(rows):
    tall, wide = grid_of(rows)
    me = lax.axis_index("rows")
    turn = lax.rem(lax.axis_index("tp"), 2) if tall == wide else 0
    return me, me // wide, lax.rem(me, wide), turn


def kernel(rows, width, step_rows, late_chunks, *refs):
    ins, gains, outs, columns = refs[:6], refs[6], refs[7:9], refs[9:11]
    late, rest = (refs[11:14], refs[14:]) if late_chunks else ((), refs[11:])
    stage, whole, peaks, gain = rest[:4]
    in_sem, peak_send, peak_recv, first_send, first_recv, next_send, next_recv = rest[4:]
    tall, wide = grid_of(rows)
    share, total = ins[0].shape
    chunks = total // width
    kept = chunks - late_chunks
    me, my_y, my_x, turn = place(rows)
    lead = (turn, 1 - turn)
    sizes = ((wide, tall), (tall, wide))

    def along_x(k):
        return my_y * wide + lax.rem(my_x + k, wide)

    def along_y(k):
        return lax.rem(my_y + k, tall) * wide + my_x

    def first_peer(m, k):
        return (1 - lead[m]) * along_x(k) + lead[m] * along_y(k)

    def next_peer(m, k):
        return (1 - lead[m]) * along_y(k) + lead[m] * along_x(k)

    def owner_next(m, j, k):
        down = (1 - lead[m]) * k + lead[m] * j
        left = (1 - lead[m]) * j + lead[m] * k
        return lax.rem(my_y + tall - down, tall) * wide + lax.rem(my_x + wide - left, wide)

    def owner_first(m, j):
        return first_peer(m, sizes[m][0] - j) if j else me

    def cols(c):
        return pl.ds(pl.multiple_of(c * width, LANES), width)

    def part(m, owner, at=None):
        rows_at = pl.ds(pl.multiple_of(owner * share, step_rows), share)
        return outs[m].at[rows_at] if at is None else outs[m].at[rows_at, at]

    def load(m, c):
        slot = lax.rem(c, 2)
        return [
            pltpu.make_async_copy(
                ins[3 * m + a].at[:, cols(c)], stage.at[slot, 3 * m + a], in_sem.at[slot, 3 * m + a]
            )
            for a in range(3)
        ]

    def send(src, dst, peer, send_sem, recv_sem):
        return pltpu.make_async_remote_copy(
            src_ref=src, dst_ref=dst, send_sem=send_sem, recv_sem=recv_sem,
            device_id={"rows": peer}, device_id_type=MESH,
        )

    def peak_copy(m, c, k, source, peer):
        slot = lax.rem(c, SLOTS)
        ref = peaks.at[m, slot, source]
        return send(ref, ref, peer, peak_send.at[m, slot, k - 1], peak_recv.at[m, slot, k - 1])

    def first_copy(m, k, src, dst, group=0):
        return send(src, dst, first_peer(m, k), first_send.at[m, k], first_recv.at[group, m, k])

    def next_copy(m, j, k, ref):
        return send(ref, ref, next_peer(m, k), next_send.at[j, m, k], next_recv.at[j, m, k])

    def last_copy():
        sems = next_send.at[1, 1, 0], next_recv.at[1, 1, 0]
        return send(late[1], late[2], next_peer(1, 1), *sems)

    for copy in load(0, 0):
        copy.start()

    barrier = pltpu.get_barrier_semaphore()
    for k in range(1, rows):
        pl.semaphore_signal(
            barrier, inc=1, device_id={"rows": lax.rem(me + k, rows)}, device_id_type=MESH
        )

    zero = (jnp.zeros((8, LANES), jnp.float32),) * (width // LANES)

    def stepped(m, slot):
        def step(i, most):
            at = pl.ds(pl.multiple_of(i * step_rows, step_rows), step_rows)
            g = gain[at, :]
            found = []
            for t in range(width // LANES):
                lane = pl.ds(t * LANES, LANES)
                train, drift, spread = (stage[slot, 3 * m + a, at, lane] for a in range(3))
                new = train - learn_rate * (
                    drift / (jnp.sqrt(spread) + tiny_value) + decay_rate * train
                )
                new = new * g
                whole[slot, m, at, lane] = new
                tops = jnp.max(jnp.abs(new).reshape(step_rows // 8, 8, LANES), axis=0)
                found.append(jnp.maximum(most[t], tops))
            return tuple(found)

        return lax.fori_loop(0, share // step_rows, step, zero)

    def share_peaks(m, c, most):
        for t in range(width // LANES):
            peaks[m, c % SLOTS, me, :, pl.ds(t * LANES, LANES)] = jnp.max(most[t], axis=0, keepdims=True)

    def send_peaks(m, c):
        for k in range(1, rows):
            peak_copy(m, c, k, me, lax.rem(me + k, rows)).start()

    def wait_peaks(m, c):
        for k in range(1, rows):
            peak_copy(m, c, k, me, lax.rem(me + k, rows)).wait_send()

    for start in range(0, share, LANES):
        count = min(LANES, share - start)
        line = gains[pl.ds(start, count)].reshape(1, count)
        gain[pl.ds(start, count), :] = jnp.broadcast_to(line, (LANES, count)).T

    for copy in load(0, 0):
        copy.wait()
    for copy in load(1, 0):
        copy.start()
    share_peaks(0, 0, stepped(0, 0))
    pl.semaphore_wait(barrier, rows - 1)
    send_peaks(0, 0)
    if chunks > 1:
        for copy in load(0, 1):
            copy.start()

    def update(m, c):
        slot = lax.rem(c, 2)
        for copy in load(m, c):
            copy.wait()

        @pl.when(c + 1 < chunks)
        def _():
            for copy in load(m, c + 1):
                copy.start()

        most = stepped(m, slot)

        @pl.when(c >= SLOTS)
        def _():
            wait_peaks(m, c - SLOTS)

        share_peaks(m, c, most)
        send_peaks(m, c)

    update(1, 0)

    def finish(m, c):
        slot = lax.rem(c, 2)
        for k in range(1, rows):
            source = lax.rem(me + rows - k, rows)
            peak_copy(m, c, k, source, source).wait_recv()
        turn_slot = lax.rem(c, SLOTS)
        scale = peaks[m, turn_slot, 0]
        for r in range(1, rows):
            scale = jnp.maximum(scale, peaks[m, turn_slot, r])
        columns[m][cols(c)] = scale[0]
        factor = 1.0 / scale

        def step(i, carry):
            at = pl.ds(pl.multiple_of(i * step_rows, step_rows), step_rows)
            to = pl.ds(pl.multiple_of(me * share + i * step_rows, step_rows), step_rows)
            outs[m][to, cols(c)] = (whole[slot, m, at, :] * factor).astype(jnp.bfloat16)
            return carry

        lax.fori_loop(0, share // step_rows, step, 0)
        own = part(m, me, cols(c))
        for k in range(1, sizes[m][0]):

            @pl.when(c < kept)
            def _(k=k):
                first_copy(m, k, own, own).start()

            if late_chunks:

                @pl.when(c >= kept)
                def _(k=k):
                    first_copy(m, k, own, late[m].at[:, cols(c - kept)], 1).start()

        for k in range(1, sizes[m][1]):
            next_copy(m, 0, k, own).start()

    def body(c, carry):
        for m in range(2):
            update(m, c)
            finish(m, c - 1)
        return carry

    lax.fori_loop(1, chunks, body, 0)
    for m in range(2):
        finish(m, chunks - 1)

    early = pl.ds(0, kept * width)
    for j in range(1, max(tall, wide)):
        for m in range(2):
            if j < sizes[m][0]:
                block = part(m, owner_first(m, j), early)
                first_copy(m, j, block, block).wait_recv()

    def relay(c, carry):
        for j in range(1, max(tall, wide)):
            for m in range(2):
                if j < sizes[m][0]:
                    for k in range(1, sizes[m][1]):
                        next_copy(m, j, k, part(m, owner_first(m, j), cols(c))).start()
        return carry

    lax.fori_loop(0, kept, relay, 0)
    if late_chunks:
        for m in (1, 0):
            first_copy(m, 1, late[m], late[m], 1).wait_recv()
            if m:
                last_copy().start()

    for m in range(2):
        for c in range(max(0, chunks - SLOTS), chunks):
            wait_peaks(m, c)
        for k in range(1, sizes[m][0]):
            first_copy(m, k, part(m, me), part(m, me)).wait_send()
        for j in range(sizes[m][0]):
            at = early if j else None
            for k in range(1, sizes[m][1]):
                next_copy(m, j, k, part(m, owner_first(m, j), at)).wait_send()
                next_copy(m, j, k, part(m, owner_next(m, j, k), at)).wait_recv()
    if late_chunks:
        last_copy().wait()


def settle(rows, late_cols, pieces, arrays, late=()):
    ins = tuple(arrays) + tuple(late)
    count = len(ins)

    def body(*refs):
        sem = refs[-1]
        copies = []

        def add(src, dst):
            copies.append(pltpu.make_async_copy(src, dst, sem.at[len(copies)]))

        for a in range(len(arrays)):
            src, dst = refs[a], refs[count + a]
            if arrays[a].ndim == 1:
                add(src, dst)
                continue
            share = arrays[a].shape[0] // rows
            tall = share // pieces
            if not late_cols:
                for p in range(rows * pieces):
                    at = pl.ds(p * tall, tall)
                    add(src.at[at], dst.at[at])
                continue
            own = arrays[a].shape[1] - late_cols
            me, near, side, far = around(rows, a)
            for owner, whole in ((me, True), (side, True), (near, False), (far, False)):
                for p in range(pieces):
                    at = pl.ds(pl.multiple_of(owner * share + p * tall, 16), tall)
                    if whole:
                        add(src.at[at], dst.at[at])
                    else:
                        add(src.at[at, pl.ds(0, own)], dst.at[at, pl.ds(0, own)])
            for owner, r in ((near, a), (far, 2))[: a + 1]:
                at = pl.ds(pl.multiple_of(owner * share, 16), share)
                add(refs[len(arrays) + r], dst.at[at, pl.ds(own, late_cols)])
        for copy in copies:
            copy.start()
        for copy in copies:
            copy.wait()

    size = sum(a.size * a.dtype.itemsize for a in arrays)
    return pl.pallas_call(
        body,
        out_shape=tuple(jax.ShapeDtypeStruct(a.shape, a.dtype) for a in arrays),
        in_specs=[pl.BlockSpec(memory_space=pl.ANY)] * count,
        out_specs=(pl.BlockSpec(memory_space=pltpu.HBM),) * len(arrays),
        scratch_shapes=[pltpu.SemaphoreType.DMA((2 * rows * pieces + 5,))],
        compiler_params=pltpu.CompilerParams(vmem_limit_bytes=SMALL),
        cost_estimate=pl.CostEstimate(flops=4 * size, bytes_accessed=2 * size, transcendentals=0),
    )(*ins)


def around(rows, m):
    me, y, x, turn = place(rows)
    turn = 1 - turn if m else turn
    by_x, by_y = y * 2 + (1 - x), (1 - y) * 2 + x
    near = (1 - turn) * by_x + turn * by_y
    side = (1 - turn) * by_y + turn * by_x
    return me, near, side, (1 - y) * 2 + (1 - x)


def complete(rows, served, piece):
    share, late_cols = piece.shape
    own = served.shape[1] - late_cols

    def body(_, src, dst, sem):
        far = around(rows, 0)[3]
        at = pl.ds(pl.multiple_of(far * share, 16), share)
        copy = pltpu.make_async_copy(src, dst.at[at, pl.ds(own, late_cols)], sem)
        copy.start()
        copy.wait()

    return pl.pallas_call(
        body,
        out_shape=jax.ShapeDtypeStruct(served.shape, served.dtype),
        in_specs=[pl.BlockSpec(memory_space=pltpu.HBM), pl.BlockSpec(memory_space=pl.ANY)],
        out_specs=pl.BlockSpec(memory_space=pltpu.HBM),
        scratch_shapes=[pltpu.SemaphoreType.DMA],
        input_output_aliases={0: 0},
        compiler_params=pltpu.CompilerParams(vmem_limit_bytes=SMALL),
    )(served, piece)


def solution(mesh):
    rows, lanes = mesh.shape["rows"], mesh.shape["tp"]

    def per_device(*args):
        arrays, norm_gain = args[:6], args[6]
        share, total = arrays[0].shape
        width = block_of(total, (LANES,))
        step_rows = block_of(share, (32, 16))
        chunks = total // width
        most = max(grid_of(rows))
        late_chunks = LATE if grid_of(rows) == (2, 2) and chunks > LATE else 0
        late_cols = late_chunks * width
        served = pltpu.VMEM((rows * share, total), jnp.bfloat16)
        column = pltpu.VMEM((total,), jnp.float32)
        late = (pltpu.VMEM((share, late_cols), jnp.bfloat16),) * 3 if late_chunks else ()
        dma = pltpu.SemaphoreType.DMA
        got = pl.pallas_call(
            functools.partial(kernel, rows, width, step_rows, late_chunks),
            out_shape=(served, served, column, column) + late,
            in_specs=[pl.BlockSpec(memory_space=pltpu.HBM)] * 6
            + [pl.BlockSpec(memory_space=pltpu.VMEM)],
            out_specs=(pl.BlockSpec(memory_space=pltpu.VMEM),) * (4 + len(late)),
            scratch_shapes=[
                pltpu.VMEM((2, 6, share, width), jnp.float32),
                pltpu.VMEM((2, 2, share, width), jnp.float32),
                pltpu.VMEM((2, SLOTS, rows, 1, width), jnp.float32),
                pltpu.VMEM((share, LANES), jnp.float32),
                dma((2, 6)),
                dma((2, SLOTS, rows - 1)),
                dma((2, SLOTS, rows - 1)),
                dma((2, most)),
                dma((2, 2, most)),
                dma((most, 2, most)),
                dma((most, 2, most)),
            ],
            compiler_params=pltpu.CompilerParams(
                collective_id=0, has_side_effects=True, vmem_limit_bytes=VMEM_LIMIT
            ),
        )(*arrays, norm_gain)
        if not late_chunks:
            return settle(rows, 0, 2, got)
        hops = [
            (r * lanes + t, (r ^ (1 if t % 2 else 2)) * lanes + t)
            for r in range(rows)
            for t in range(lanes)
        ]
        piece = lax.ppermute(got[4], ("rows", "tp"), hops)
        done = settle(rows, late_cols, 2, got[:4], got[4:])
        return (complete(rows, done[0], piece),) + tuple(done[1:])

    split = P("rows", "tp")
    return jax.shard_map(
        per_device,
        mesh=mesh,
        in_specs=(split,) * 6 + (P("rows"),),
        out_specs=(P(None, "tp"), P(None, "tp"), P("tp"), P("tp")),
        check_vma=False,
    )


LATE = 4
SLOTS = 4
VMEM_LIMIT = 30 * 1024 * 1024
SMALL = 1024 * 1024
```

time: 227 us -> 222 us (0.978)
  Pallas kernels: 220 us -> 216 us
    pallas_call x1, Pallas kernels: 211 us -> 206 us  [per_device(): pl.pallas_call(functools.partial(kernel, rows, width, step_rows, late_chu...]
where the time goes in v2:
time: 222 us; the launch traced here: 221 us
  Pallas kernels  216 us (97%)
  waiting for transfers between devices  2.94 us (1%)
    pallas_call x1, Pallas kernels, per_device(): pl.pallas_call(functools.partial(kernel, rows, width, step_rows, late_chu...  206 us
    pallas_call x1, Pallas kernels, settle(): pl.pallas_call(body, out_shape=tuple((jax.ShapeDtypeStruct(a.shape, a.dty...  8.42 us
  transfers between devices with their start and end apart: 1, of which 1 were waited for; matrix products, arithmetic and copies ran while one was open for 0% of the time, Pallas kernels for 4%

profile of v2, /device:TPU:1, one launch (start us, length us, event | category | flops | bytes accessed | tf_op | source)
XLA Modules:
  0.0 220.7 jit_solution(17752703299840869815)
XLA Ops:
  0.6 206.5 %shard_map.102 = (bf16[3584,1792]{1,0:T(8,128)(2,1)S(1)}, bf16[3584,1792]{1,0:T(8,128)(2,1)S(1)}, f32[1792]{0:T(1024)S(1)}, f32[1792]{0:T(1024)S(1)}, bf16[896,5...) custom-call(f32[896,1792]{1,0:T(8,128)} %refs_0_.1, f32[896,1792]{1,0:T(8,128)} %refs_1_.1, ...), custom_call_target="tpu_custom_call" | custom-call | tf_op jit(solution)/shard_map/pallas_call | solution.py:363
  207.1 1.2 collective-permute-start
  208.4 8.4 %shard_map.103 = (bf16[3584,1792]{1,0:T(8,128)(2,1)}, bf16[3584,1792]{1,0:T(8,128)(2,1)}, f32[1792]{0:T(1024)}, f32[1792]{0:T(1024)}) custom-call(bf16[3584,1792]{1,0:T(8,128)(2,1)S(1)} %get-tuple-element.15.refs_0_, bf16[3584,1792]{1,0:T(8,128)(2,1)S(1)} %get-tuple-element.16.refs_1_, f32[1792]{0:T(1024)S(1)} %get-tuple-element.17.refs_2_, ...), custom_call_target="tpu_custom_call" | custom-call | flops 102817792 | bytes 51408896 | tf_op jit(solution)/shard_map/pallas_call | solution.py:305
  216.8 2.9 %collective-permute-done.src = bf16[896,512]{1,0:T(8,128)(2,1)S(1)} collective-permute-done((bf16[896,512]{1,0:T(8,128)(2,1)S(1)}, bf16[896,512]{1,0:T(8,128)(2,1)S(1)}, u32[]{:S(2)}, u32[]{:S(2)}) %collective-permute-start) | collective-permute-done | bytes 917536 | tf_op jit(solution)/shard_map/ppermute | solution.py:393
  219.7 0.9 shard_map.104
Async XLA Ops:
  207.1 12.6 %collective-permute-start = (bf16[896,512]{1,0:T(8,128)(2,1)S(1)}, bf16[896,512]{1,0:T(8,128)(2,1)S(1)}, u32[]{:S(2)}, u32[]{:S(2)}) collective-permute-start(bf16[896,512]{1,0:T(8,128)(2,1)S(1)} %get-tuple-element.19.refs_4_), channel_id=1, source_target_pairs={{0,16},{1,9},{2,18},{3,11},{4,20},{5,13},{6,22},{7,15},{8,24},{9,1... | collective-permute-start | bytes 2752520 | tf_op jit(solution)/shard_map/ppermute | solution.py:393

commit v3 on v2

--- a/solution.py
+++ b/solution.py
@@ -31,16 +31,20 @@
     return me, me // wide, lax.rem(me, wide), turn
 
 
-def kernel(rows, width, step_rows, late_chunks, *refs):
+def kernel(rows, width, step_rows, held, gone, *refs):
     ins, gains, outs, columns = refs[:6], refs[6], refs[7:9], refs[9:11]
-    late, rest = (refs[11:14], refs[14:]) if late_chunks else ((), refs[11:])
+    sides, rest = (refs[11:17], refs[17:]) if gone else ((), refs[11:])
+    near, far, late = sides[:2], sides[2:4], sides[4:]
     stage, whole, peaks, gain = rest[:4]
-    in_sem, peak_send, peak_recv, first_send, first_recv, next_send, next_recv = rest[4:]
+    in_sem, peak_send, peak_recv, first_send, first_recv, next_send, next_recv = rest[4:11]
+    if gone:
+        held_send, held_recv, go = rest[11:]
     tall, wide = grid_of(rows)
     share, total = ins[0].shape
     chunks = total // width
-    kept = chunks - late_chunks
+    kept = chunks - held - gone
     me, my_y, my_x, turn = place(rows)
+    tp = lax.axis_index("tp")
     lead = (turn, 1 - turn)
     sizes = ((wide, tall), (tall, wide))
 
@@ -71,14 +75,23 @@
         rows_at = pl.ds(pl.multiple_of(owner * share, step_rows), share)
         return outs[m].at[rows_at] if at is None else outs[m].at[rows_at, at]
 
-    def load(m, c):
+    def load(m, c, pieces=1):
         slot = lax.rem(c, 2)
+        tall_piece = share // pieces
         return [
             pltpu.make_async_copy(
-                ins[3 * m + a].at[:, cols(c)], stage.at[slot, 3 * m + a], in_sem.at[slot, 3 * m + a]
+                ins[3 * m + a].at[pl.ds(p * tall_piece, tall_piece), cols(c)],
+                stage.at[slot, 3 * m + a, pl.ds(p * tall_piece, tall_piece)],
+                in_sem.at[slot, m],
             )
+            for p in range(pieces)
             for a in range(3)
         ]
+
+    def wait_load(m, c):
+        slot = lax.rem(c, 2)
+        block = stage.at[slot, pl.ds(3 * m, 3)]
+        pltpu.make_async_copy(block, block, in_sem.at[slot, m]).wait()
 
     def send(src, dst, peer, send_sem, recv_sem):
         return pltpu.make_async_remote_copy(
@@ -86,22 +99,29 @@
             device_id={"rows": peer}, device_id_type=MESH,
         )
 
-    def peak_copy(m, c, k, source, peer):
+    def peak_copy(m, c, k):
         slot = lax.rem(c, SLOTS)
-        ref = peaks.at[m, slot, source]
-        return send(ref, ref, peer, peak_send.at[m, slot, k - 1], peak_recv.at[m, slot, k - 1])
+        ref = peaks.at[m, slot, me]
+        return send(ref, ref, lax.rem(me + k, rows), peak_send.at[m, slot], peak_recv.at[m, slot])
+
+    def all_peaks(m, c):
+        slot = lax.rem(c, SLOTS)
+        ref = peaks.at[m, slot, pl.ds(0, rows - 1)]
+        return send(ref, ref, lax.rem(me + 1, rows), peak_send.at[m, slot], peak_recv.at[m, slot])
 
     def first_copy(m, k, src, dst, group=0):
-        return send(src, dst, first_peer(m, k), first_send.at[m, k], first_recv.at[group, m, k])
+        sems = first_send.at[m, k - 1], first_recv.at[group, m, k - 1]
+        return send(src, dst, first_peer(m, k), *sems)
 
     def next_copy(m, j, k, ref):
-        return send(ref, ref, next_peer(m, k), next_send.at[j, m, k], next_recv.at[j, m, k])
-
-    def last_copy():
-        sems = next_send.at[1, 1, 0], next_recv.at[1, 1, 0]
-        return send(late[1], late[2], next_peer(1, 1), *sems)
-
-    for copy in load(0, 0):
+        return send(ref, ref, next_peer(m, k), next_send.at[j, m, k - 1], next_recv.at[j, m, k - 1])
+
+    def held_copy(m, half):
+        at = pl.ds(half * (share // 2), share // 2)
+        sems = held_send.at[m, half], held_recv.at[m, half]
+        return send(near[m].at[at], far[m].at[at], next_peer(m, 1), *sems)
+
+    for copy in load(0, 0, block_of(share, (7, 1)) if share % 112 == 0 else 1):
         copy.start()
 
     barrier = pltpu.get_barrier_semaphore()
@@ -109,6 +129,10 @@
         pl.semaphore_signal(
             barrier, inc=1, device_id={"rows": lax.rem(me + k, rows)}, device_id_type=MESH
         )
+
+    if gone:
+        sibling = {"tp": tp + 1 - 2 * turn}
+        pl.semaphore_signal(barrier, inc=1, device_id=sibling, device_id_type=MESH)
 
     zero = (jnp.zeros((8, LANES), jnp.float32),) * (width // LANES)
 
@@ -137,23 +161,18 @@
 
     def send_peaks(m, c):
         for k in range(1, rows):
-            peak_copy(m, c, k, me, lax.rem(me + k, rows)).start()
-
-    def wait_peaks(m, c):
-        for k in range(1, rows):
-            peak_copy(m, c, k, me, lax.rem(me + k, rows)).wait_send()
+            peak_copy(m, c, k).start()
 
     for start in range(0, share, LANES):
         count = min(LANES, share - start)
         line = gains[pl.ds(start, count)].reshape(1, count)
         gain[pl.ds(start, count), :] = jnp.broadcast_to(line, (LANES, count)).T
 
-    for copy in load(0, 0):
-        copy.wait()
+    wait_load(0, 0)
     for copy in load(1, 0):
         copy.start()
     share_peaks(0, 0, stepped(0, 0))
-    pl.semaphore_wait(barrier, rows - 1)
+    pl.semaphore_wait(barrier, rows if gone else rows - 1)
     send_peaks(0, 0)
     if chunks > 1:
         for copy in load(0, 1):
@@ -161,8 +180,7 @@
 
     def update(m, c):
         slot = lax.rem(c, 2)
-        for copy in load(m, c):
-            copy.wait()
+        wait_load(m, c)
 
         @pl.when(c + 1 < chunks)
         def _():
@@ -173,7 +191,7 @@
 
         @pl.when(c >= SLOTS)
         def _():
-            wait_peaks(m, c - SLOTS)
+            all_peaks(m, c - SLOTS).wait_send()
 
         share_peaks(m, c, most)
         send_peaks(m, c)
@@ -182,9 +200,7 @@
 
     def finish(m, c):
         slot = lax.rem(c, 2)
-        for k in range(1, rows):
-            source = lax.rem(me + rows - k, rows)
-            peak_copy(m, c, k, source, source).wait_recv()
+        all_peaks(m, c).wait_recv()
         turn_slot = lax.rem(c, SLOTS)
         scale = peaks[m, turn_slot, 0]
         for r in range(1, rows):
@@ -206,11 +222,15 @@
             def _(k=k):
                 first_copy(m, k, own, own).start()
 
-            if late_chunks:
-
-                @pl.when(c >= kept)
+            if gone:
+
+                @pl.when((c >= kept) & (c < kept + held))
                 def _(k=k):
-                    first_copy(m, k, own, late[m].at[:, cols(c - kept)], 1).start()
+                    first_copy(m, k, own, near[m].at[:, cols(c - kept)], 1).start()
+
+                @pl.when(c >= kept + held)
+                def _(k=k):
+                    first_copy(m, k, own, late[m].at[:, cols(c - kept - held)], 2).start()
 
         for k in range(1, sizes[m][1]):
             next_copy(m, 0, k, own).start()
@@ -241,15 +261,30 @@
         return carry
 
     lax.fori_loop(0, kept, relay, 0)
-    if late_chunks:
-        for m in (1, 0):
-            first_copy(m, 1, late[m], late[m], 1).wait_recv()
-            if m:
-                last_copy().start()
+    if gone:
+        for m in range(2):
+            first_copy(m, 1, near[m], near[m], 1).wait_recv()
+
+        @pl.when(turn == 1)
+        def _():
+            pl.semaphore_wait(go, 1)
+
+        for half in range(2):
+            for m in range(2):
+                held_copy(m, half).start()
+        for m in range(2):
+            held_copy(m, 0).wait_send()
+
+        @pl.when(turn == 0)
+        def _():
+            pl.semaphore_signal(go, inc=1, device_id=sibling, device_id_type=MESH)
+
+        for m in range(2):
+            first_copy(m, 1, late[m], late[m], 2).wait_recv()
 
     for m in range(2):
         for c in range(max(0, chunks - SLOTS), chunks):
-            wait_peaks(m, c)
+            all_peaks(m, c).wait_send()
         for k in range(1, sizes[m][0]):
             first_copy(m, k, part(m, me), part(m, me)).wait_send()
         for j in range(sizes[m][0]):
@@ -257,16 +292,20 @@
             for k in range(1, sizes[m][1]):
                 next_copy(m, j, k, part(m, owner_first(m, j), at)).wait_send()
                 next_copy(m, j, k, part(m, owner_next(m, j, k), at)).wait_recv()
-    if late_chunks:
-        last_copy().wait()
-
-
-def settle(rows, late_cols, pieces, arrays, late=()):
-    ins = tuple(arrays) + tuple(late)
+    if gone:
+        for m in range(2):
+            held_copy(m, 1).wait_send()
+            for half in range(2):
+                held_copy(m, half).wait_recv()
+
+
+def settle(rows, held_cols, late_cols, pieces, arrays, sides=()):
+    ins = tuple(arrays) + tuple(sides)
     count = len(ins)
 
     def body(*refs):
         sem = refs[-1]
+        near, far, late = refs[4:6], refs[6:8], refs[8:10]
         copies = []
 
         def add(src, dst):
@@ -284,18 +323,20 @@
                     at = pl.ds(p * tall, tall)
                     add(src.at[at], dst.at[at])
                 continue
-            own = arrays[a].shape[1] - late_cols
-            me, near, side, far = around(rows, a)
-            for owner, whole in ((me, True), (side, True), (near, False), (far, False)):
+            own = arrays[a].shape[1] - late_cols - held_cols
+            me, first, second, last = around(rows, a)
+            for owner, whole in ((me, True), (second, True), (first, False), (last, False)):
                 for p in range(pieces):
                     at = pl.ds(pl.multiple_of(owner * share + p * tall, 16), tall)
                     if whole:
                         add(src.at[at], dst.at[at])
                     else:
                         add(src.at[at, pl.ds(0, own)], dst.at[at, pl.ds(0, own)])
-            for owner, r in ((near, a), (far, 2))[: a + 1]:
-                at = pl.ds(pl.multiple_of(owner * share, 16), share)
-                add(refs[len(arrays) + r], dst.at[at, pl.ds(own, late_cols)])
+            first_at = pl.ds(pl.multiple_of(first * share, 16), share)
+            last_at = pl.ds(pl.multiple_of(last * share, 16), share)
+            add(near[a], dst.at[first_at, pl.ds(own, held_cols)])
+            add(late[a], dst.at[first_at, pl.ds(own + held_cols, late_cols)])
+            add(far[a], dst.at[last_at, pl.ds(own, held_cols)])
         for copy in copies:
             copy.start()
         for copy in copies:
@@ -307,7 +348,7 @@
         out_shape=tuple(jax.ShapeDtypeStruct(a.shape, a.dtype) for a in arrays),
         in_specs=[pl.BlockSpec(memory_space=pl.ANY)] * count,
         out_specs=(pl.BlockSpec(memory_space=pltpu.HBM),) * len(arrays),
-        scratch_shapes=[pltpu.SemaphoreType.DMA((2 * rows * pieces + 5,))],
+        scratch_shapes=[pltpu.SemaphoreType.DMA((2 * rows * pieces + 8,))],
         compiler_params=pltpu.CompilerParams(vmem_limit_bytes=SMALL),
         cost_estimate=pl.CostEstimate(flops=4 * size, bytes_accessed=2 * size, transcendentals=0),
     )(*ins)
@@ -322,26 +363,32 @@
     return me, near, side, (1 - y) * 2 + (1 - x)
 
 
-def complete(rows, served, piece):
-    share, late_cols = piece.shape
-    own = served.shape[1] - late_cols
-
-    def body(_, src, dst, sem):
-        far = around(rows, 0)[3]
-        at = pl.ds(pl.multiple_of(far * share, 16), share)
-        copy = pltpu.make_async_copy(src, dst.at[at, pl.ds(own, late_cols)], sem)
-        copy.start()
-        copy.wait()
+def complete(rows, served, late):
+    share, late_cols = late[0].shape
+    own = served[0].shape[1] - late_cols
+
+    def body(*refs):
+        sem = refs[-1]
+        copies = []
+        for m in range(2):
+            at = pl.ds(pl.multiple_of(around(rows, m)[3] * share, 16), share)
+            dst = refs[4 + m].at[at, pl.ds(own, late_cols)]
+            copies.append(pltpu.make_async_copy(refs[2 + m], dst, sem.at[m]))
+        for copy in copies:
+            copy.start()
+        for copy in copies:
+            copy.wait()
 
     return pl.pallas_call(
         body,
-        out_shape=jax.ShapeDtypeStruct(served.shape, served.dtype),
-        in_specs=[pl.BlockSpec(memory_space=pltpu.HBM), pl.BlockSpec(memory_space=pl.ANY)],
-        out_specs=pl.BlockSpec(memory_space=pltpu.HBM),
-        scratch_shapes=[pltpu.SemaphoreType.DMA],
-        input_output_aliases={0: 0},
+        out_shape=tuple(jax.ShapeDtypeStruct(a.shape, a.dtype) for a in served),
+        in_specs=[pl.BlockSpec(memory_space=pltpu.HBM)] * 2
+        + [pl.BlockSpec(memory_space=pl.ANY)] * 2,
+        out_specs=(pl.BlockSpec(memory_space=pltpu.HBM),) * 2,
+        scratch_shapes=[pltpu.SemaphoreType.DMA((2,))],
+        input_output_aliases={0: 0, 1: 1},
         compiler_params=pltpu.CompilerParams(vmem_limit_bytes=SMALL),
-    )(served, piece)
+    )(*served, *late)
 
 
 def solution(mesh):
@@ -354,45 +401,55 @@
         step_rows = block_of(share, (32, 16))
         chunks = total // width
         most = max(grid_of(rows))
-        late_chunks = LATE if grid_of(rows) == (2, 2) and chunks > LATE else 0
-        late_cols = late_chunks * width
+        split = grid_of(rows) == (2, 2) and lanes % 2 == 0 and chunks > HELD + LATE
+        held, gone = (HELD, LATE) if split else (0, 0)
         served = pltpu.VMEM((rows * share, total), jnp.bfloat16)
         column = pltpu.VMEM((total,), jnp.float32)
-        late = (pltpu.VMEM((share, late_cols), jnp.bfloat16),) * 3 if late_chunks else ()
+        sides = ()
         dma = pltpu.SemaphoreType.DMA
+        more = []
+        if split:
+            held_side = pltpu.VMEM((share, held * width), jnp.bfloat16)
+            sides = (held_side,) * 4 + (pltpu.VMEM((share, gone * width), jnp.bfloat16),) * 2
+            more = [dma((2, 2)), dma((2, 2)), pltpu.SemaphoreType.REGULAR]
         got = pl.pallas_call(
-            functools.partial(kernel, rows, width, step_rows, late_chunks),
-            out_shape=(served, served, column, column) + late,
+            functools.partial(kernel, rows, width, step_rows, held, gone),
+            out_shape=(served, served, column, column) + sides,
             in_specs=[pl.BlockSpec(memory_space=pltpu.HBM)] * 6
             + [pl.BlockSpec(memory_space=pltpu.VMEM)],
-            out_specs=(pl.BlockSpec(memory_space=pltpu.VMEM),) * (4 + len(late)),
+            out_specs=(pl.BlockSpec(memory_space=pltpu.VMEM),) * (4 + len(sides)),
             scratch_shapes=[
                 pltpu.VMEM((2, 6, share, width), jnp.float32),
                 pltpu.VMEM((2, 2, share, width), jnp.float32),
                 pltpu.VMEM((2, SLOTS, rows, 1, width), jnp.float32),
                 pltpu.VMEM((share, LANES), jnp.float32),
-                dma((2, 6)),
-                dma((2, SLOTS, rows - 1)),
-                dma((2, SLOTS, rows - 1)),
-                dma((2, most)),
-                dma((2, 2, most)),
-                dma((most, 2, most)),
-                dma((most, 2, most)),
-            ],
+                dma((2, 2)),
+                dma((2, SLOTS)),
+                dma((2, SLOTS)),
+                dma((2, most - 1)),
+                dma((3 if split else 1, 2, most - 1)),
+                dma((most, 2, most - 1)),
+                dma((most, 2, most - 1)),
+            ]
+            + more,
             compiler_params=pltpu.CompilerParams(
                 collective_id=0, has_side_effects=True, vmem_limit_bytes=VMEM_LIMIT
             ),
         )(*arrays, norm_gain)
-        if not late_chunks:
-            return settle(rows, 0, 2, got)
-        hops = [
-            (r * lanes + t, (r ^ (1 if t % 2 else 2)) * lanes + t)
-            for r in range(rows)
-            for t in range(lanes)
-        ]
-        piece = lax.ppermute(got[4], ("rows", "tp"), hops)
-        done = settle(rows, late_cols, 2, got[:4], got[4:])
-        return (complete(rows, done[0], piece),) + tuple(done[1:])
+        if not split:
+            return settle(rows, 0, 0, 2, got)
+
+        def hop(m, late):
+            hops = [
+                (r * lanes + t, (r ^ (1 if (t + m) % 2 else 2)) * lanes + t)
+                for r in range(rows)
+                for t in range(lanes)
+            ]
+            return lax.ppermute(late, ("rows", "tp"), hops)
+
+        late = [hop(m, got[8 + m]) for m in range(2)]
+        done = settle(rows, held * width, gone * width, 2, got[:4], got[4:])
+        return tuple(complete(rows, done[:2], late)) + tuple(done[2:])
 
     split = P("rows", "tp")
     return jax.shard_map(
@@ -404,7 +461,8 @@
     )
 
 
-LATE = 4
+HELD = 2
+LATE = 3
 SLOTS = 4
 VMEM_LIMIT = 30 * 1024 * 1024
 SMALL = 1024 * 1024

time: 222 us -> 219 us (0.986)
  Pallas kernels: 216 us -> 210 us
  waiting for transfers between devices: 2.94 us -> 6.67 us
    pallas_call x2, Pallas kernels: 207 us -> 202 us  [the longest x1 201 us: per_device(): pl.pallas_call(functools.partial(kernel, rows, width, step_rows, held, go...]
    ppermute x1 -> x2, waiting for transfers between devices: 2.94 us -> 6.67 us  [hop(): return lax.ppermute(late, ('rows', 'tp'), hops)]
  transfers between devices with their start and end apart: 1 -> 2, of which waited for: 1 -> 1; matrix products, arithmetic and copies ran while one was open for 0% -> 0% of each run, Pallas kernels for 4% -> 4%
where the time goes in v3:
time: 219 us
  Pallas kernels  210 us (96%)
  waiting for transfers between devices  6.67 us (3%)
    pallas_call x1, Pallas kernels, per_device(): pl.pallas_call(functools.partial(kernel, rows, width, step_rows, held, go...  201 us
    pallas_call x1, Pallas kernels, settle(): pl.pallas_call(body, out_shape=tuple((jax.ShapeDtypeStruct(a.shape, a.dty...  8.29 us
    ppermute x2, waiting for transfers between devices, hop(): return lax.ppermute(late, ('rows', 'tp'), hops)  6.67 us
  transfers between devices with their start and end apart: 2, of which 1 were waited for; matrix products, arithmetic and copies ran while one was open for 0% of the time, Pallas kernels for 4%

profile of v3, /device:TPU:1, one launch (start us, length us, event | category | flops | bytes accessed | tf_op | source)
XLA Modules:
  0.0 219.2 jit_solution(9786285914571178718)
XLA Ops:
  0.6 200.9 %shard_map.102 = (bf16[3584,1792]{1,0:T(8,128)(2,1)S(1)}, bf16[3584,1792]{1,0:T(8,128)(2,1)S(1)}, f32[1792]{0:T(1024)S(1)}, f32[1792]{0:T(1024)S(1)}, bf16[896,2...) custom-call(f32[896,1792]{1,0:T(8,128)} %refs_0_.1, ...), custom_call_target="tpu_custom_call" | custom-call | tf_op jit(solution)/shard_map/pallas_call | solution.py:415
  201.6 1.3 collective-permute-start
  202.9 0.3 collective-permute-start.1
  203.1 8.3 %shard_map.103 = (bf16[3584,1792]{1,0:T(8,128)(2,1)}, bf16[3584,1792]{1,0:T(8,128)(2,1)}, f32[1792]{0:T(1024)}, f32[1792]{0:T(1024)}) custom-call(bf16[3584,1792]{1,0:T(8,128)(2,1)S(1)} %get-tuple-element.20.refs_0_, bf16[3584,1792]{1,0:T(8,128)(2,1)S(1)} %get-tuple-element.21.refs_1_, f32[1792]{0:T(1024)S(1)} %get-tuple-element.22.refs_2_, ...), custom_call_target="tpu_custom_call" | custom-call | flops 102817792 | bytes 51408896 | tf_op jit(solution)/shard_map/pallas_call | solution.py:346
  211.4 6.7 %collective-permute-done.refs_2_ = bf16[896,384]{1,0:T(8,128)(2,1)S(1)} collective-permute-done((bf16[896,384]{1,0:T(8,128)(2,1)S(1)}, bf16[896,384]{1,0:T(8,128)(2,1)S(1)}, u32[]{:S(2)}, u32[]{:S(2)}) %collective-permute-start) | collective-permute-done | bytes 688160 | tf_op jit(solution)/shard_map/ppermute | solution.py:448
  218.1 0.0 collective-permute-done.1.refs_3_
  218.1 1.1 shard_map.104
Async XLA Ops:
  201.6 16.5 %collective-permute-start = (bf16[896,384]{1,0:T(8,128)(2,1)S(1)}, bf16[896,384]{1,0:T(8,128)(2,1)S(1)}, u32[]{:S(2)}, u32[]{:S(2)}) collective-permute-start(bf16[896,384]{1,0:T(8,128)(2,1)S(1)} %get-tuple-element.28.refs_8_), channel_id=1, source_target_pairs={{0,16},{1,9},{2,18},{3,11},{4,20},{5,13},{6,22},{7,15},{8,24},{9,1... | collective-permute-start | bytes 2064392 | tf_op jit(solution)/shard_map/ppermute | solution.py:448
  202.9 15.3 %collective-permute-start.1 = (bf16[896,384]{1,0:T(8,128)(2,1)S(1)}, bf16[896,384]{1,0:T(8,128)(2,1)S(1)}, u32[]{:S(2)}, u32[]{:S(2)}) collective-permute-start(bf16[896,384]{1,0:T(8,128)(2,1)S(1)} %get-tuple-element.29.refs_9_), channel_id=1, source_target_pairs={{0,8},{1,17},{2,10},{3,19},{4,12},{5,21},{6,14},{7,23},{8,0},{9,25... | collective-permute-start | bytes 2064392 | tf_op jit(solution)/shard_map/ppermute | solution.py:448

commit v4 on v3

--- a/solution.py
+++ b/solution.py
@@ -36,9 +36,10 @@
     sides, rest = (refs[11:17], refs[17:]) if gone else ((), refs[11:])
     near, far, late = sides[:2], sides[2:4], sides[4:]
     stage, whole, peaks, gain = rest[:4]
-    in_sem, peak_send, peak_recv, first_send, first_recv, next_send, next_recv = rest[4:11]
-    if gone:
-        held_send, held_recv, go = rest[11:]
+    in_sem, piece_sem, peak_send, peak_recv = rest[4:8]
+    first_send, first_recv, next_send, next_recv = rest[8:12]
+    if gone:
+        held_send, held_recv, go, early, early_send, early_recv, rest_send, rest_recv = rest[12:]
     tall, wide = grid_of(rows)
     share, total = ins[0].shape
     chunks = total // width
@@ -71,20 +72,15 @@
     def cols(c):
         return pl.ds(pl.multiple_of(c * width, LANES), width)
 
-    def part(m, owner, at=None):
-        rows_at = pl.ds(pl.multiple_of(owner * share, step_rows), share)
-        return outs[m].at[rows_at] if at is None else outs[m].at[rows_at, at]
-
-    def load(m, c, pieces=1):
+    def part(m, owner, at):
+        return outs[m].at[pl.ds(pl.multiple_of(owner * share, step_rows), share), at]
+
+    def load(m, c):
         slot = lax.rem(c, 2)
-        tall_piece = share // pieces
         return [
             pltpu.make_async_copy(
-                ins[3 * m + a].at[pl.ds(p * tall_piece, tall_piece), cols(c)],
-                stage.at[slot, 3 * m + a, pl.ds(p * tall_piece, tall_piece)],
-                in_sem.at[slot, m],
+                ins[3 * m + a].at[:, cols(c)], stage.at[slot, 3 * m + a], in_sem.at[slot, m]
             )
-            for p in range(pieces)
             for a in range(3)
         ]
 
@@ -121,8 +117,25 @@
         sems = held_send.at[m, half], held_recv.at[m, half]
         return send(near[m].at[at], far[m].at[at], next_peer(m, 1), *sems)
 
-    for copy in load(0, 0, block_of(share, (7, 1)) if share % 112 == 0 else 1):
-        copy.start()
+    def early_copy(side):
+        src, dst = whole.at[0, 0, pl.ds(0, EARLY)], early.at[side]
+        peer = (first_peer, next_peer)[side](0, 1)
+        return send(src, dst, peer, early_send.at[side], early_recv.at[side])
+
+    def rest_copy(side, owner):
+        at = pl.ds(pl.multiple_of(owner * share + EARLY, step_rows), share - EARLY)
+        ref = outs[0].at[at, cols(0)]
+        peer = (first_peer, next_peer)[side](0, 1)
+        return send(ref, ref, peer, rest_send.at[side], rest_recv.at[side])
+
+    pieces = piece_sem.shape[0]
+    tall_piece = share // pieces
+    for p in range(pieces):
+        at = pl.ds(p * tall_piece, tall_piece)
+        for a in range(3):
+            pltpu.make_async_copy(
+                ins[a].at[at, cols(0)], stage.at[0, a, at], piece_sem.at[p]
+            ).start()
 
     barrier = pltpu.get_barrier_semaphore()
     for k in range(1, rows):
@@ -136,7 +149,7 @@
 
     zero = (jnp.zeros((8, LANES), jnp.float32),) * (width // LANES)
 
-    def stepped(m, slot):
+    def stepped(m, slot, low, high, most):
         def step(i, most):
             at = pl.ds(pl.multiple_of(i * step_rows, step_rows), step_rows)
             g = gain[at, :]
@@ -153,7 +166,7 @@
                 found.append(jnp.maximum(most[t], tops))
             return tuple(found)
 
-        return lax.fori_loop(0, share // step_rows, step, zero)
+        return lax.fori_loop(low // step_rows, high // step_rows, step, most)
 
     def share_peaks(m, c, most):
         for t in range(width // LANES):
@@ -168,12 +181,20 @@
         line = gains[pl.ds(start, count)].reshape(1, count)
         gain[pl.ds(start, count), :] = jnp.broadcast_to(line, (LANES, count)).T
 
-    wait_load(0, 0)
-    for copy in load(1, 0):
-        copy.start()
-    share_peaks(0, 0, stepped(0, 0))
+    most = zero
+    for p in range(pieces):
+        block = stage.at[0, pl.ds(0, 3), pl.ds(p * tall_piece, tall_piece)]
+        pltpu.make_async_copy(block, block, piece_sem.at[p]).wait()
+        if p == pieces // 2:
+            for copy in load(1, 0):
+                copy.start()
+        most = stepped(0, 0, p * tall_piece, (p + 1) * tall_piece, most)
+    share_peaks(0, 0, most)
     pl.semaphore_wait(barrier, rows if gone else rows - 1)
     send_peaks(0, 0)
+    if gone:
+        for side in range(2):
+            early_copy(side).start()
     if chunks > 1:
         for copy in load(0, 1):
             copy.start()
@@ -187,7 +208,7 @@
             for copy in load(m, c + 1):
                 copy.start()
 
-        most = stepped(m, slot)
+        most = stepped(m, slot, 0, share, zero)
 
         @pl.when(c >= SLOTS)
         def _():
@@ -198,7 +219,7 @@
 
     update(1, 0)
 
-    def finish(m, c):
+    def finish(m, c, split=False):
         slot = lax.rem(c, 2)
         all_peaks(m, c).wait_recv()
         turn_slot = lax.rem(c, SLOTS)
@@ -215,6 +236,10 @@
             return carry
 
         lax.fori_loop(0, share // step_rows, step, 0)
+        if split:
+            for side in range(2):
+                rest_copy(side, me).start()
+            return
         own = part(m, me, cols(c))
         for k in range(1, sizes[m][0]):
 
@@ -241,15 +266,43 @@
             finish(m, c - 1)
         return carry
 
-    lax.fori_loop(1, chunks, body, 0)
+    if gone:
+        update(0, 1)
+        finish(0, 0, True)
+        update(1, 1)
+        finish(1, 0)
+        for side in range(2):
+            early_copy(side).wait_send()
+    lax.fori_loop(2 if gone else 1, chunks, body, 0)
     for m in range(2):
         finish(m, chunks - 1)
 
-    early = pl.ds(0, kept * width)
+    apart = width if gone else 0
+
+    def span(m, j):
+        low = apart if j == 0 and m == 0 else 0
+        high = total if j == 0 else kept * width
+        return pl.ds(low, high - low)
+
+    if gone:
+        factor = 1.0 / columns[0][cols(0)].reshape(1, width)
+        for side in range(2):
+            owner = (first_peer, next_peer)[side](0, 1)
+            early_copy(side).wait_recv()
+
+            def scale_step(i, carry, side=side, owner=owner):
+                at = pl.ds(pl.multiple_of(i * step_rows, step_rows), step_rows)
+                to = pl.ds(pl.multiple_of(owner * share + i * step_rows, step_rows), step_rows)
+                outs[0][to, cols(0)] = (early[side, at, :] * factor).astype(jnp.bfloat16)
+                return carry
+
+            lax.fori_loop(0, EARLY // step_rows, scale_step, 0)
+        rest_copy(0, first_peer(0, 1)).wait_recv()
     for j in range(1, max(tall, wide)):
         for m in range(2):
             if j < sizes[m][0]:
-                block = part(m, owner_first(m, j), early)
+                at = pl.ds(0 if m else apart, kept * width - (0 if m else apart))
+                block = part(m, owner_first(m, j), at)
                 first_copy(m, j, block, block).wait_recv()
 
     def relay(c, carry):
@@ -286,14 +339,17 @@
         for c in range(max(0, chunks - SLOTS), chunks):
             all_peaks(m, c).wait_send()
         for k in range(1, sizes[m][0]):
-            first_copy(m, k, part(m, me), part(m, me)).wait_send()
+            own = part(m, me, span(m, 0))
+            first_copy(m, k, own, own).wait_send()
         for j in range(sizes[m][0]):
-            at = early if j else None
+            at = span(m, j)
             for k in range(1, sizes[m][1]):
                 next_copy(m, j, k, part(m, owner_first(m, j), at)).wait_send()
                 next_copy(m, j, k, part(m, owner_next(m, j, k), at)).wait_recv()
     if gone:
-        for m in range(2):
+        rest_copy(1, next_peer(0, 1)).wait_recv()
+        for m in range(2):
+            rest_copy(m, me).wait_send()
             held_copy(m, 1).wait_send()
             for half in range(2):
                 held_copy(m, half).wait_recv()
@@ -401,7 +457,9 @@
         step_rows = block_of(share, (32, 16))
         chunks = total // width
         most = max(grid_of(rows))
-        split = grid_of(rows) == (2, 2) and lanes % 2 == 0 and chunks > HELD + LATE
+        split = grid_of(rows) == (2, 2) and lanes % 2 == 0
+        split = split and chunks > HELD + LATE and share > EARLY and EARLY % step_rows == 0
+        pieces = 7 if share % (7 * step_rows) == 0 else 1
         held, gone = (HELD, LATE) if split else (0, 0)
         served = pltpu.VMEM((rows * share, total), jnp.bfloat16)
         column = pltpu.VMEM((total,), jnp.float32)
@@ -412,6 +470,7 @@
             held_side = pltpu.VMEM((share, held * width), jnp.bfloat16)
             sides = (held_side,) * 4 + (pltpu.VMEM((share, gone * width), jnp.bfloat16),) * 2
             more = [dma((2, 2)), dma((2, 2)), pltpu.SemaphoreType.REGULAR]
+            more += [pltpu.VMEM((2, EARLY, width), jnp.float32)] + [dma((2,))] * 4
         got = pl.pallas_call(
             functools.partial(kernel, rows, width, step_rows, held, gone),
             out_shape=(served, served, column, column) + sides,
@@ -424,6 +483,7 @@
                 pltpu.VMEM((2, SLOTS, rows, 1, width), jnp.float32),
                 pltpu.VMEM((share, LANES), jnp.float32),
                 dma((2, 2)),
+                dma((pieces,)),
                 dma((2, SLOTS)),
                 dma((2, SLOTS)),
                 dma((2, most - 1)),
@@ -461,7 +521,8 @@
     )
 
 
-HELD = 2
+HELD = 3
+EARLY = 256
 LATE = 3
 SLOTS = 4
 VMEM_LIMIT = 30 * 1024 * 1024

time: 219 us -> 217 us (level)
  no operation moved by 1% of the time
where the time goes in v4:
time: 217 us
  Pallas kernels  210 us (97%)
  waiting for transfers between devices  4.78 us (2%)
    pallas_call x1, Pallas kernels, per_device(): pl.pallas_call(functools.partial(kernel, rows, width, step_rows, held, go...  200 us
    pallas_call x1, Pallas kernels, settle(): pl.pallas_call(body, out_shape=tuple((jax.ShapeDtypeStruct(a.shape, a.dty...  8.3 us
    ppermute x2, waiting for transfers between devices, hop(): return lax.ppermute(late, ('rows', 'tp'), hops)  4.78 us
  transfers between devices with their start and end apart: 2, of which 1 were waited for; matrix products, arithmetic and copies ran while one was open for 0% of the time, Pallas kernels for 4%

profile of v4, /device:TPU:1, one launch (start us, length us, event | category | flops | bytes accessed | tf_op | source)
XLA Modules:
  0.0 216.6 jit_solution(10134111650669980721)
XLA Ops:
  0.6 200.3 %shard_map.102 = (bf16[3584,1792]{1,0:T(8,128)(2,1)S(1)}, bf16[3584,1792]{1,0:T(8,128)(2,1)S(1)}, f32[1792]{0:T(1024)S(1)}, f32[1792]{0:T(1024)S(1)}, bf16[896,3...) custom-call(f32[896,1792]{1,0:T(8,128)} %refs_0_.1, ...), custom_call_target="tpu_custom_call" | custom-call | tf_op jit(solution)/shard_map/pallas_call | solution.py:474
  201.0 1.3 collective-permute-start
  202.2 0.2 collective-permute-start.1
  202.5 8.3 %shard_map.103 = (bf16[3584,1792]{1,0:T(8,128)(2,1)}, bf16[3584,1792]{1,0:T(8,128)(2,1)}, f32[1792]{0:T(1024)}, f32[1792]{0:T(1024)}) custom-call(bf16[3584,1792]{1,0:T(8,128)(2,1)S(1)} %get-tuple-element.20.refs_0_, bf16[3584,1792]{1,0:T(8,128)(2,1)S(1)} %get-tuple-element.21.refs_1_, f32[1792]{0:T(1024)S(1)} %get-tuple-element.22.refs_2_, ...), custom_call_target="tpu_custom_call" | custom-call | flops 102817792 | bytes 51408896 | tf_op jit(solution)/shard_map/pallas_call | solution.py:402
  210.8 4.8 %collective-permute-done.refs_2_ = bf16[896,384]{1,0:T(8,128)(2,1)S(1)} collective-permute-done((bf16[896,384]{1,0:T(8,128)(2,1)S(1)}, bf16[896,384]{1,0:T(8,128)(2,1)S(1)}, u32[]{:S(2)}, u32[]{:S(2)}) %collective-permute-start) | collective-permute-done | bytes 688160 | tf_op jit(solution)/shard_map/ppermute | solution.py:508
  215.5 0.0 collective-permute-done.1.refs_3_
  215.5 1.1 shard_map.104
Async XLA Ops:
  201.0 14.6 %collective-permute-start = (bf16[896,384]{1,0:T(8,128)(2,1)S(1)}, bf16[896,384]{1,0:T(8,128)(2,1)S(1)}, u32[]{:S(2)}, u32[]{:S(2)}) collective-permute-start(bf16[896,384]{1,0:T(8,128)(2,1)S(1)} %get-tuple-element.28.refs_8_), channel_id=1, source_target_pairs={{0,16},{1,9},{2,18},{3,11},{4,20},{5,13},{6,22},{7,15},{8,24},{9,1... | collective-permute-start | bytes 2064392 | tf_op jit(solution)/shard_map/ppermute | solution.py:508
  202.2 13.3 %collective-permute-start.1 = (bf16[896,384]{1,0:T(8,128)(2,1)S(1)}, bf16[896,384]{1,0:T(8,128)(2,1)S(1)}, u32[]{:S(2)}, u32[]{:S(2)}) collective-permute-start(bf16[896,384]{1,0:T(8,128)(2,1)S(1)} %get-tuple-element.29.refs_9_), channel_id=1, source_target_pairs={{0,8},{1,17},{2,10},{3,19},{4,12},{5,21},{6,14},{7,23},{8,0},{9,25... | collective-permute-start | bytes 2064392 | tf_op jit(solution)/shard_map/ppermute | solution.py:508

commit v5 on v4

--- a/solution.py
+++ b/solution.py
@@ -113,8 +113,8 @@
         return send(ref, ref, next_peer(m, k), next_send.at[j, m, k - 1], next_recv.at[j, m, k - 1])
 
     def held_copy(m, half):
-        at = pl.ds(half * (share // 2), share // 2)
-        sems = held_send.at[m, half], held_recv.at[m, half]
+        at = pl.ds(0, share) if half is None else pl.ds(half * (share // 2), share // 2)
+        sems = held_send.at[m, half or 0], held_recv.at[m, half or 0]
         return send(near[m].at[at], far[m].at[at], next_peer(m, 1), *sems)
 
     def early_copy(side):
@@ -321,15 +321,16 @@
         @pl.when(turn == 1)
         def _():
             pl.semaphore_wait(go, 1)
-
-        for half in range(2):
             for m in range(2):
-                held_copy(m, half).start()
-        for m in range(2):
-            held_copy(m, 0).wait_send()
+                held_copy(m, None).start()
 
         @pl.when(turn == 0)
         def _():
+            for half in range(2):
+                for m in range(2):
+                    held_copy(m, half).start()
+            for m in range(2):
+                held_copy(m, 0).wait_send()
             pl.semaphore_signal(go, inc=1, device_id=sibling, device_id_type=MESH)
 
         for m in range(2):
@@ -350,9 +351,18 @@
         rest_copy(1, next_peer(0, 1)).wait_recv()
         for m in range(2):
             rest_copy(m, me).wait_send()
-            held_copy(m, 1).wait_send()
-            for half in range(2):
-                held_copy(m, half).wait_recv()
+
+        @pl.when(turn == 0)
+        def _():
+            for m in range(2):
+                held_copy(m, 1).wait_send()
+                for half in range(2):
+                    held_copy(m, half).wait_recv()
+
+        @pl.when(turn == 1)
+        def _():
+            for m in range(2):
+                held_copy(m, None).wait()
 
 
 def settle(rows, held_cols, late_cols, pieces, arrays, sides=()):
@@ -521,9 +531,9 @@
     )
 
 
-HELD = 3
+HELD = 4
 EARLY = 256
 LATE = 3
 SLOTS = 4
-VMEM_LIMIT = 30 * 1024 * 1024
+VMEM_LIMIT = 31 * 1024 * 1024
 SMALL = 1024 * 1024

time: 217 us -> 216 us (level)
  waiting for transfers between devices: 4.78 us -> 2.47 us
    ppermute x2, waiting for transfers between devices: 4.78 us -> 2.47 us  [hop(): return lax.ppermute(late, ('rows', 'tp'), hops)]
where the time goes in v5:
time: 216 us
  Pallas kernels  211 us (98%)
  waiting for transfers between devices  2.47 us (1%)
    pallas_call x1, Pallas kernels, per_device(): pl.pallas_call(functools.partial(kernel, rows, width, step_rows, held, go...  202 us
    pallas_call x1, Pallas kernels, settle(): pl.pallas_call(body, out_shape=tuple((jax.ShapeDtypeStruct(a.shape, a.dty...  8.3 us
  transfers between devices with their start and end apart: 2, of which 1 were waited for; matrix products, arithmetic and copies ran while one was open for 0% of the time, Pallas kernels for 4%

profile of v5, /device:TPU:1, one launch (start us, length us, event | category | flops | bytes accessed | tf_op | source)
XLA Modules:
  0.0 215.6 jit_solution(16301855822356730626)
XLA Ops:
  0.6 201.6 %shard_map.102 = (bf16[3584,1792]{1,0:T(8,128)(2,1)S(1)}, bf16[3584,1792]{1,0:T(8,128)(2,1)S(1)}, f32[1792]{0:T(1024)S(1)}, f32[1792]{0:T(1024)S(1)}, bf16[896,5...) custom-call(f32[896,1792]{1,0:T(8,128)} %refs_0_.1, ...), custom_call_target="tpu_custom_call" | custom-call | tf_op jit(solution)/shard_map/pallas_call | solution.py:484
  202.2 1.3 collective-permute-start
  203.5 0.2 collective-permute-start.1
  203.7 8.3 %shard_map.103 = (bf16[3584,1792]{1,0:T(8,128)(2,1)}, bf16[3584,1792]{1,0:T(8,128)(2,1)}, f32[1792]{0:T(1024)}, f32[1792]{0:T(1024)}) custom-call(bf16[3584,1792]{1,0:T(8,128)(2,1)S(1)} %get-tuple-element.20.refs_0_, bf16[3584,1792]{1,0:T(8,128)(2,1)S(1)} %get-tuple-element.21.refs_1_, f32[1792]{0:T(1024)S(1)} %get-tuple-element.22.refs_2_, ...), custom_call_target="tpu_custom_call" | custom-call | flops 102817792 | bytes 51408896 | tf_op jit(solution)/shard_map/pallas_call | solution.py:412
  212.0 2.4 %collective-permute-done.refs_2_ = bf16[896,384]{1,0:T(8,128)(2,1)S(1)} collective-permute-done((bf16[896,384]{1,0:T(8,128)(2,1)S(1)}, bf16[896,384]{1,0:T(8,128)(2,1)S(1)}, u32[]{:S(2)}, u32[]{:S(2)}) %collective-permute-start) | collective-permute-done | bytes 688160 | tf_op jit(solution)/shard_map/ppermute | solution.py:518
  214.4 0.0 collective-permute-done.1.refs_3_
  214.5 1.1 shard_map.104
Async XLA Ops:
  202.2 12.2 %collective-permute-start = (bf16[896,384]{1,0:T(8,128)(2,1)S(1)}, bf16[896,384]{1,0:T(8,128)(2,1)S(1)}, u32[]{:S(2)}, u32[]{:S(2)}) collective-permute-start(bf16[896,384]{1,0:T(8,128)(2,1)S(1)} %get-tuple-element.28.refs_8_), channel_id=1, source_target_pairs={{0,16},{1,9},{2,18},{3,11},{4,20},{5,13},{6,22},{7,15},{8,24},{9,1... | collective-permute-start | bytes 2064392 | tf_op jit(solution)/shard_map/ppermute | solution.py:518
  203.5 11.0 %collective-permute-start.1 = (bf16[896,384]{1,0:T(8,128)(2,1)S(1)}, bf16[896,384]{1,0:T(8,128)(2,1)S(1)}, u32[]{:S(2)}, u32[]{:S(2)}) collective-permute-start(bf16[896,384]{1,0:T(8,128)(2,1)S(1)} %get-tuple-element.29.refs_9_), channel_id=1, source_target_pairs={{0,8},{1,17},{2,10},{3,19},{4,12},{5,21},{6,14},{7,23},{8,0},{9,25... | collective-permute-start | bytes 2064392 | tf_op jit(solution)/shard_map/ppermute | solution.py:518

commit v6 on v5

--- a/solution.py
+++ b/solution.py
@@ -128,6 +128,16 @@
         peer = (first_peer, next_peer)[side](0, 1)
         return send(ref, ref, peer, rest_send.at[side], rest_recv.at[side])
 
+    barrier = pltpu.get_barrier_semaphore()
+    for k in range(1, rows):
+        pl.semaphore_signal(
+            barrier, inc=1, device_id={"rows": lax.rem(me + k, rows)}, device_id_type=MESH
+        )
+
+    if gone:
+        sibling = {"tp": tp + 1 - 2 * turn}
+        pl.semaphore_signal(barrier, inc=1, device_id=sibling, device_id_type=MESH)
+
     pieces = piece_sem.shape[0]
     tall_piece = share // pieces
     for p in range(pieces):
@@ -136,16 +146,6 @@
             pltpu.make_async_copy(
                 ins[a].at[at, cols(0)], stage.at[0, a, at], piece_sem.at[p]
             ).start()
-
-    barrier = pltpu.get_barrier_semaphore()
-    for k in range(1, rows):
-        pl.semaphore_signal(
-            barrier, inc=1, device_id={"rows": lax.rem(me + k, rows)}, device_id_type=MESH
-        )
-
-    if gone:
-        sibling = {"tp": tp + 1 - 2 * turn}
-        pl.semaphore_signal(barrier, inc=1, device_id=sibling, device_id_type=MESH)
 
     zero = (jnp.zeros((8, LANES), jnp.float32),) * (width // LANES)
 
@@ -468,7 +468,7 @@
         chunks = total // width
         most = max(grid_of(rows))
         split = grid_of(rows) == (2, 2) and lanes % 2 == 0
-        split = split and chunks > HELD + LATE and share > EARLY and EARLY % step_rows == 0
+        split = split and chunks > HELD + LATE + 1 and share > EARLY and EARLY % step_rows == 0
         pieces = 7 if share % (7 * step_rows) == 0 else 1
         held, gone = (HELD, LATE) if split else (0, 0)
         served = pltpu.VMEM((rows * share, total), jnp.bfloat16)

time: 216 us -> 216 us (level)
  no operation moved by 1% of the time
where the time goes in v6:
time: 216 us
  Pallas kernels  211 us (98%)
  waiting for transfers between devices  2.47 us (1%)
    pallas_call x1, Pallas kernels, per_device(): pl.pallas_call(functools.partial(kernel, rows, width, step_rows, held, go...  202 us
    pallas_call x1, Pallas kernels, settle(): pl.pallas_call(body, out_shape=tuple((jax.ShapeDtypeStruct(a.shape, a.dty...  8.3 us
  transfers between devices with their start and end apart: 2, of which 1 were waited for; matrix products, arithmetic and copies ran while one was open for 0% of the time, Pallas kernels for 4%

profile of v6, /device:TPU:1, one launch (start us, length us, event | category | flops | bytes accessed | tf_op | source)
XLA Modules:
  0.0 215.6 jit_solution(8640965180392530027)
XLA Ops:
  0.6 201.6 %shard_map.102 = (bf16[3584,1792]{1,0:T(8,128)(2,1)S(1)}, bf16[3584,1792]{1,0:T(8,128)(2,1)S(1)}, f32[1792]{0:T(1024)S(1)}, f32[1792]{0:T(1024)S(1)}, bf16[896,5...) custom-call(f32[896,1792]{1,0:T(8,128)} %refs_0_.1, ...), custom_call_target="tpu_custom_call" | custom-call | tf_op jit(solution)/shard_map/pallas_call | solution.py:484
  202.2 1.3 collective-permute-start
  203.5 0.2 collective-permute-start.1
  203.7 8.3 %shard_map.103 = (bf16[3584,1792]{1,0:T(8,128)(2,1)}, bf16[3584,1792]{1,0:T(8,128)(2,1)}, f32[1792]{0:T(1024)}, f32[1792]{0:T(1024)}) custom-call(bf16[3584,1792]{1,0:T(8,128)(2,1)S(1)} %get-tuple-element.20.refs_0_, bf16[3584,1792]{1,0:T(8,128)(2,1)S(1)} %get-tuple-element.21.refs_1_, f32[1792]{0:T(1024)S(1)} %get-tuple-element.22.refs_2_, ...), custom_call_target="tpu_custom_call" | custom-call | flops 102817792 | bytes 51408896 | tf_op jit(solution)/shard_map/pallas_call | solution.py:412
  212.0 2.4 %collective-permute-done.refs_2_ = bf16[896,384]{1,0:T(8,128)(2,1)S(1)} collective-permute-done((bf16[896,384]{1,0:T(8,128)(2,1)S(1)}, bf16[896,384]{1,0:T(8,128)(2,1)S(1)}, u32[]{:S(2)}, u32[]{:S(2)}) %collective-permute-start) | collective-permute-done | bytes 688160 | tf_op jit(solution)/shard_map/ppermute | solution.py:518
  214.4 0.0 collective-permute-done.1.refs_3_
  214.5 1.1 shard_map.104
Async XLA Ops:
  202.2 12.2 %collective-permute-start = (bf16[896,384]{1,0:T(8,128)(2,1)S(1)}, bf16[896,384]{1,0:T(8,128)(2,1)S(1)}, u32[]{:S(2)}, u32[]{:S(2)}) collective-permute-start(bf16[896,384]{1,0:T(8,128)(2,1)S(1)} %get-tuple-element.28.refs_8_), channel_id=1, source_target_pairs={{0,16},{1,9},{2,18},{3,11},{4,20},{5,13},{6,22},{7,15},{8,24},{9,1... | collective-permute-start | bytes 2064392 | tf_op jit(solution)/shard_map/ppermute | solution.py:518
  203.5 11.0 %collective-permute-start.1 = (bf16[896,384]{1,0:T(8,128)(2,1)S(1)}, bf16[896,384]{1,0:T(8,128)(2,1)S(1)}, u32[]{:S(2)}, u32[]{:S(2)}) collective-permute-start(bf16[896,384]{1,0:T(8,128)(2,1)S(1)} %get-tuple-element.29.refs_9_), channel_id=1, source_target_pairs={{0,8},{1,17},{2,10},{3,19},{4,12},{5,21},{6,14},{7,23},{8,0},{9,25... | collective-permute-start | bytes 2064392 | tf_op jit(solution)/shard_map/ppermute | solution.py:518

commit v7 on v6

--- a/solution.py
+++ b/solution.py
@@ -158,7 +158,7 @@
                 lane = pl.ds(t * LANES, LANES)
                 train, drift, spread = (stage[slot, 3 * m + a, at, lane] for a in range(3))
                 new = train - learn_rate * (
-                    drift / (jnp.sqrt(spread) + tiny_value) + decay_rate * train
+                    drift / (spread * lax.rsqrt(spread) + tiny_value) + decay_rate * train
                 )
                 new = new * g
                 whole[slot, m, at, lane] = new
@@ -235,11 +235,13 @@
             outs[m][to, cols(c)] = (whole[slot, m, at, :] * factor).astype(jnp.bfloat16)
             return carry
 
-        lax.fori_loop(0, share // step_rows, step, 0)
         if split:
+            lax.fori_loop(EARLY // step_rows, share // step_rows, step, 0)
             for side in range(2):
                 rest_copy(side, me).start()
+            lax.fori_loop(0, EARLY // step_rows, step, 0)
             return
+        lax.fori_loop(0, share // step_rows, step, 0)
         own = part(m, me, cols(c))
         for k in range(1, sizes[m][0]):
 

time: 216 us -> 216 us (level)
  no operation moved by 1% of the time
where the time goes in v7:
time: 216 us
  Pallas kernels  211 us (98%)
  waiting for transfers between devices  2.47 us (1%)
    pallas_call x1, Pallas kernels, per_device(): pl.pallas_call(functools.partial(kernel, rows, width, step_rows, held, go...  202 us
    pallas_call x1, Pallas kernels, settle(): pl.pallas_call(body, out_shape=tuple((jax.ShapeDtypeStruct(a.shape, a.dty...  8.3 us
  transfers between devices with their start and end apart: 2, of which 1 were waited for; matrix products, arithmetic and copies ran while one was open for 0% of the time, Pallas kernels for 4%

profile of v7, /device:TPU:1, one launch (start us, length us, event | category | flops | bytes accessed | tf_op | source)
XLA Modules:
  0.0 215.5 jit_solution(15581583853425373174)
XLA Ops:
  0.6 201.5 %shard_map.102 = (bf16[3584,1792]{1,0:T(8,128)(2,1)S(1)}, bf16[3584,1792]{1,0:T(8,128)(2,1)S(1)}, f32[1792]{0:T(1024)S(1)}, f32[1792]{0:T(1024)S(1)}, bf16[896,5...) custom-call(f32[896,1792]{1,0:T(8,128)} %refs_0_.1, ...), custom_call_target="tpu_custom_call" | custom-call | tf_op jit(solution)/shard_map/pallas_call | solution.py:486
  202.2 1.3 collective-permute-start
  203.4 0.2 collective-permute-start.1
  203.7 8.3 %shard_map.103 = (bf16[3584,1792]{1,0:T(8,128)(2,1)}, bf16[3584,1792]{1,0:T(8,128)(2,1)}, f32[1792]{0:T(1024)}, f32[1792]{0:T(1024)}) custom-call(bf16[3584,1792]{1,0:T(8,128)(2,1)S(1)} %get-tuple-element.20.refs_0_, bf16[3584,1792]{1,0:T(8,128)(2,1)S(1)} %get-tuple-element.21.refs_1_, f32[1792]{0:T(1024)S(1)} %get-tuple-element.22.refs_2_, ...), custom_call_target="tpu_custom_call" | custom-call | flops 102817792 | bytes 51408896 | tf_op jit(solution)/shard_map/pallas_call | solution.py:414
  212.0 2.4 %collective-permute-done.refs_2_ = bf16[896,384]{1,0:T(8,128)(2,1)S(1)} collective-permute-done((bf16[896,384]{1,0:T(8,128)(2,1)S(1)}, bf16[896,384]{1,0:T(8,128)(2,1)S(1)}, u32[]{:S(2)}, u32[]{:S(2)}) %collective-permute-start) | collective-permute-done | bytes 688160 | tf_op jit(solution)/shard_map/ppermute | solution.py:520
  214.4 0.0 collective-permute-done.1.refs_3_
  214.4 1.1 shard_map.104
Async XLA Ops:
  202.2 12.2 %collective-permute-start = (bf16[896,384]{1,0:T(8,128)(2,1)S(1)}, bf16[896,384]{1,0:T(8,128)(2,1)S(1)}, u32[]{:S(2)}, u32[]{:S(2)}) collective-permute-start(bf16[896,384]{1,0:T(8,128)(2,1)S(1)} %get-tuple-element.28.refs_8_), channel_id=1, source_target_pairs={{0,16},{1,9},{2,18},{3,11},{4,20},{5,13},{6,22},{7,15},{8,24},{9,1... | collective-permute-start | bytes 2064392 | tf_op jit(solution)/shard_map/ppermute | solution.py:520
  203.4 11.0 %collective-permute-start.1 = (bf16[896,384]{1,0:T(8,128)(2,1)S(1)}, bf16[896,384]{1,0:T(8,128)(2,1)S(1)}, u32[]{:S(2)}, u32[]{:S(2)}) collective-permute-start(bf16[896,384]{1,0:T(8,128)(2,1)S(1)} %get-tuple-element.29.refs_9_), channel_id=1, source_target_pairs={{0,8},{1,17},{2,10},{3,19},{4,12},{5,21},{6,14},{7,23},{8,0},{9,25... | collective-permute-start | bytes 2064392 | tf_op jit(solution)/shard_map/ppermute | solution.py:520
